TPU v7x, 512 devices: a whole 4x8x8 slice. The times are simulated.
512 devices in a mesh: leaf: 256 (over z, y, x), blk: 2 (over core).
Axes of the slice: x: 4, y: 8, z: 8, core: 2. Of those that a mesh axis runs over, the one named last changes fastest.
Arguments:
- sketch: bfloat16 [262144, 512], P(('leaf', 'blk')), may hold values from -6 to 6
- near_block: bfloat16 [262144, 1024], P(('leaf', 'blk')), may hold values from -0.125 to 0.125
- next_block: bfloat16 [262144, 1024], P(('leaf', 'blk')), may hold values from -0.125 to 0.125
- link_own: bfloat16 [65536, 1024], P('leaf', 'blk')
- link_next: bfloat16 [65536, 1024], P('leaf', 'blk')
- diag_block: float32 [65536, 128], P(('leaf', 'blk'))
- sub_block: float32 [65536, 128], P(('leaf', 'blk'))
- leaf_skeleton: int32 [256, 128], P('leaf'), may hold values from 0 to 1023, as said below
- merge_skeleton: int32 [256, 4, 128], P('leaf'), may hold values from 0 to 255, as said below
Outputs:
- samples: float32 [262144, 512], P(('leaf', 'blk'))
- leaf_interp: float32 [262144, 128], P(('leaf', 'blk'))
- merge_interp: float32 [512, 4, 256, 128], P(('leaf', 'blk'))
Inputs may be any that keep to these rules, and one draw needn't show every extreme that they name: `leaf_skeleton`: each row holds 128 distinct numbers. `merge_skeleton`: for each row p and level index j, the 128 numbers are distinct; rows p and q with p // 2^(j+1) == q // 2^(j+1) hold equal entries at level index j.
All inputs are finite; a program needn't handle non-finite values.
Results may differ from a plain program's by a relative error of at most 0.0027.
Values may be sent and summed in bfloat16 or wider, within the bound.
No kernel may reach another device: no remote copies, remote signals or barrier semaphores. Data moves between devices by JAX's collectives and lax.ppermute only.
A program may use at most 64 MiB of HBM per device.

v0:
```python
import jax
import jax.numpy as jnp
from jax import lax
from jax.experimental import pallas as pl
from jax.experimental.pallas import tpu as pltpu
from jax.sharding import Mesh, PartitionSpec as P

f32 = jnp.float32
bf16 = jnp.bfloat16
highest = lax.Precision.HIGHEST
STEP = 16
NN = (((1,), (0,)), ((), ()))
NT = (((1,), (1,)), ((), ()))


def dot1(a, b, dims=NN):
    return lax.dot_general(a, b, dims, preferred_element_type=f32)


def dot6(a, b, dims=NN):
    return lax.dot_general(a, b, dims, preferred_element_type=f32, precision=highest)


def halves(a):
    high = a.astype(bf16)
    return high, (a - high.astype(f32)).astype(bf16)


def dot3(a, b, dims=NN):
    (ah, al), (bh, bl) = halves(a), halves(b)
    return dot1(ah, bh, dims) + (dot1(ah, bl, dims) + dot1(al, bh, dims))


def iota(shape, dim):
    return lax.broadcasted_iota(jnp.int32, shape, dim)


def lane_columns(packed):
    first = iota(packed.shape, 1) // STEP * STEP
    return [
        jnp.take_along_axis(packed, first + j, axis=1, mode="promise_in_bounds")
        for j in range(STEP)
    ]


def lane_packed(columns):
    at = iota(columns[0].shape, 1) % STEP
    parts = [jnp.where(at == j, c, 0.0) for j, c in enumerate(columns)]
    while len(parts) > 1:
        parts = [a + b for a, b in zip(parts[::2], parts[1::2])]
    return parts[0]


def group_inverse(packed):
    columns = lane_columns(packed)
    row = iota(packed.shape, 0)
    scale = jnp.ones_like(packed)
    for k in range(STEP):
        here = row == k
        inv = 1.0 / columns[k][k : k + 1]
        scale = jnp.where(here, inv, scale)
        multiple = jnp.where(here, 0.0, columns[k] * inv)
        columns = [
            jnp.where(here, 1.0, -multiple) if j == k else c - multiple * c[k : k + 1]
            for j, c in enumerate(columns)
        ]
    return lane_packed([c * scale for c in columns])


def group_lower_inverse(packed):
    columns = lane_columns(packed)
    row = iota(packed.shape, 0)
    x = jnp.where(row == iota(packed.shape, 1) % STEP, 1.0, 0.0)
    for k in range(STEP):
        pivot = x[k : k + 1] / columns[k][k : k + 1]
        below = jnp.where(row > k, columns[k], 0.0)
        x = jnp.where(row == k, pivot, x - below * pivot)
    return x


def block_rows(packed):
    size = packed.shape[1]
    same = iota((size, size), 0) // STEP == iota((size, size), 1) // STEP
    return jnp.where(same, jnp.concatenate([packed] * (size // STEP), axis=0), 0.0)


def lower_inverse(lower):
    size = lower.shape[0]
    group = iota((STEP, size), 1) // STEP
    packed = jnp.zeros((STEP, size), f32)
    for q in range(size // STEP):
        packed = jnp.where(group == q, lower[q * STEP : (q + 1) * STEP], packed)
    x = block_rows(group_lower_inverse(packed))
    row, col = iota((size, size), 0), iota((size, size), 1)
    width = STEP
    while width < size:
        pair = (row // width == col // width + 1) & (col // width % 2 == 0)
        x = x - dot6(x, dot6(jnp.where(pair, lower, 0.0), x))
        width *= 2
    return x


def factor_body(blocks, inverse, transposed):
    size = blocks.shape[2]
    low = iota((size, size), 0) >= iota((size, size), 1)
    first = lower_inverse(jnp.where(low, blocks[0, :size], 0.0))
    last = lower_inverse(jnp.where(low, blocks[1, :size], 0.0))
    corner = -dot6(last, dot6(blocks[1, size:], first))
    inverse[:size, :size] = first
    inverse[:size, size:] = jnp.zeros((size, size), f32)
    inverse[size:, :size] = corner
    inverse[size:, size:] = last
    transposed[...] = inverse[...].T


def solve_body(own, others, inverse, transposed, weights):
    load = own[...] + others[...]
    weights[...] = dot6(transposed[...], dot6(inverse[...], load)).astype(bf16)


def samples_body(direct, link, weights, pick, samples, chosen):
    width = weights.shape[2]
    for c in range(weights.shape[0]):
        at = pl.ds(c * width, width)
        part = direct[:, at] - dot1(link[...], weights[c])
        samples[:, at] = part
        high, low = halves(part)
        count = pick.shape[0]
        chosen[:count, at] = dot1(pick[...], high).astype(bf16)
        chosen[count:, at] = dot1(pick[...], low).astype(bf16)


def turned(rows, by):
    return jnp.concatenate([rows[rows.shape[0] - by :], rows[: rows.shape[0] - by]], axis=0) if by else rows


def invert_all(gram, count, size):
    groups = size // STEP
    group = iota((STEP, size), 1) // STEP
    wide_group = iota((size, size), 1) // STEP
    same = iota((size, size), 0) // STEP == wide_group
    unit = jnp.where(iota((STEP, size), 0) == iota((STEP, size), 1) % STEP, 1.0, 0.0)
    for k in range(groups):
        rows = pl.ds(k * STEP, STEP)
        panels = [gram[g, rows, :] for g in range(count)]
        packed = unit
        for g in range(count):
            packed = jnp.where(group == (k + g) % groups, panels[g], packed)
        pivots = block_rows(group_inverse(packed))
        stacked = [
            panels[(q - k) % groups] if (q - k) % groups < count else jnp.zeros((STEP, size), f32)
            for q in range(groups)
        ]
        scaled = dot3(pivots, jnp.concatenate(stacked, axis=0))
        scaled = jnp.where(same, pivots, scaled)
        left = jnp.concatenate(
            [jnp.where(wide_group == (k + g) % groups, gram[g], 0.0) for g in range(count)], axis=0
        )
        change = dot3(left, scaled)
        for g in range(count):
            q = (k + g) % groups
            gram[g] = jnp.where(wide_group == q, 0.0, gram[g]) - change[g * size : (g + 1) * size]
            gram[g, rows, :] = scaled[q * STEP : (q + 1) * STEP]


def interp_body(samples, leaf, *refs):
    levels = (len(refs) - 3) // 2
    candidates, chosen = refs[:levels], refs[levels : 2 * levels]
    leaf_interp, merge_interp, gram = refs[2 * levels :]
    size = chosen[0].shape[0]
    high, low = leaf[:size], leaf[size:]
    yh, yl = halves(samples[...])
    cross = [dot1(yh, high, NT) + (dot1(yh, low, NT) + dot1(yl, high, NT))]
    gram[0] = dot1(high, high, NT) + (dot1(high, low, NT) + dot1(low, high, NT))
    for j in range(levels):
        rows = chosen[j][...]
        spun = turned(rows, STEP * (j + 1))
        gram[j + 1] = dot1(rows, spun, NT)
        cross.append(dot1(candidates[j][...], spun, NT))
    invert_all(gram, levels + 1, size)
    leaf_interp[...] = dot3(cross[0], gram[0], NT)
    for j in range(levels):
        merge_interp[0, j] = dot3(cross[j + 1], gram[j + 1], NT)


def call(body, outs, *args, scratch=()):
    shapes = tuple(jax.ShapeDtypeStruct(s, t) for s, t in outs)
    return pl.pallas_call(
        body,
        out_shape=shapes if len(shapes) > 1 else shapes[0],
        scratch_shapes=list(scratch),
        name=body.__name__,
    )(*args)


def solution(mesh):
    leaf_count, blk_count = mesh.shape["leaf"], mesh.shape["blk"]
    bits = ("b3", "b2", "b1", "b0")
    names = ("top", *bits, "blk")
    fine = Mesh(mesh.devices.reshape(leaf_count >> 4, 2, 2, 2, 2, blk_count), names)
    leaf = names[:-1]

    def shifted(block, distance):
        route = [((i - distance) % leaf_count, i) for i in range(leaf_count)]
        return lax.ppermute(block, leaf, route)

    def swapped(block):
        return lax.ppermute(block, "blk", [(0, 1), (1, 0)])

    def both(block):
        return lax.all_gather(block, "blk", axis=0)

    def per_device(
        sketch, near_block, next_block, link_own, link_next, diag_block, sub_block, leaf_set, merge_sets
    ):
        here = lax.axis_index("blk")
        rows, cols = sketch.shape
        interior = link_own.shape[0]
        rank = leaf_set.shape[1]
        half = cols // 2

        next_half = shifted(sketch, -1)
        previous_link = shifted(link_next, 1)
        other_half = swapped(sketch)
        factors = both(jnp.concatenate([diag_block, sub_block], axis=0))
        inverse, transposed = call(
            factor_body, [((interior, interior), f32)] * 2, factors
        )

        def times_whole(matrix, own, other):
            mine = lax.dynamic_slice_in_dim(matrix, here * rows, rows, 1)
            theirs = lax.dynamic_slice_in_dim(matrix, (1 - here) * rows, rows, 1)
            return dot1(mine, own) + dot1(theirs, other)

        near_part = times_whole(near_block, sketch, other_half)
        load = dot1(link_own, sketch) + dot1(link_next, next_half)
        sent = lax.dynamic_slice_in_dim(load, (1 - here) * half, half, 1)
        kept = lax.dynamic_slice_in_dim(load, here * half, half, 1)
        got = lax.dynamic_index_in_dim(both(sent), 1 - here, 0, keepdims=False)
        weights = call(
            solve_body, [((interior, half), bf16)], kept, got, inverse, transposed
        )
        previous_weights = shifted(weights, 1)
        next_other = swapped(next_half)
        all_weights = both(weights)
        direct = near_part + times_whole(next_block, next_half, next_other)
        own_link = link_own.T
        direct = direct - jnp.concatenate(
            [dot1(own_link, all_weights[c]) for c in range(2)], axis=1
        )
        all_previous = both(previous_weights)
        pick = (
            leaf_set[0][:, None] == here * rows + jnp.arange(rows, dtype=jnp.int32)[None]
        ).astype(bf16)
        samples, picked = call(
            samples_body,
            [((rows, cols), f32), ((2 * rank, cols), bf16)],
            direct,
            previous_link.T,
            all_previous,
            pick,
        )
        pieces = both(picked)
        leaf_rows = pieces[0] + pieces[1]
        chosen = leaf_rows[:rank]
        candidates, kept_rows = [], []
        for level, axis in enumerate(reversed(bits)):
            pair = lax.all_gather(chosen, axis, axis=0, tiled=True)
            pick = (
                merge_sets[0, level][:, None] == jnp.arange(2 * rank, dtype=jnp.int32)[None]
            ).astype(bf16)
            chosen = dot1(pick, pair).astype(bf16)
            candidates.append(pair)
            kept_rows.append(chosen)
        levels = len(candidates)
        leaf_interp, merge_interp = call(
            interp_body,
            [((rows, rank), f32), ((1, levels, 2 * rank, rank), f32)],
            samples,
            leaf_rows,
            *candidates,
            *kept_rows,
            scratch=[pltpu.VMEM((levels + 1, rank, rank), f32)],
        )
        return samples, leaf_interp, merge_interp

    split = P((*leaf, "blk"), None)
    linked = P(leaf, "blk")
    return jax.shard_map(
        per_device,
        mesh=fine,
        in_specs=(split, split, split, linked, linked, split, split, P(leaf, None), P(leaf, None, None)),
        out_specs=(split, split, P((*leaf, "blk"), None, None, None)),
        check_vma=False,
    )
```

profile of v0, /device:TPU:2, one launch (start us, length us, event | category | flops | bytes accessed | tf_op | source)
XLA Modules:
  0.0 99.5 jit_solution(15097241720355360504)
XLA Ops:
  0.7 2.1 %collective-permute-start = (bf16[512,512]{1,0:T(8,128)(2,1)}, bf16[512,512]{1,0:T(8,128)(2,1)}, u32[]{:S(2)}, u32[]{:S(2)}) collective-permute-start(bf16[512,512]{1,0:T(8,128)(2,1)} %param.9), channel_id=1, source_target_pairs={{0,1},{1,0},{2,3},{3,2},{4,5},{5,4},{6,7},{7,6},{8,9},{9,8},{10,11... | collective-permute-start | bytes 1572872 | tf_op jit(solution)/shard_map/ppermute | solution.py:208
  2.7 7.8 %collective-permute-start.1 = (bf16[512,512]{1,0:T(8,128)(2,1)}, bf16[512,512]{1,0:T(8,128)(2,1)S(1)}, u32[]{:S(2)}, u32[]{:S(2)}) collective-permute-start(bf16[512,512]{1,0:T(8,128)(2,1)} %param.9), channel_id=1, source_target_pairs={{2,0},{4,2},{6,4},{8,6},{10,8},{12,10},{14,12},{16,14},{18,16},{20... | collective-permute-start | bytes 1572872 | tf_op jit(solution)/shard_map/ppermute | solution.py:205
  10.5 1.8 %copy.14 = bf16[256,512]{0,1:T(8,128)(2,1)} copy(bf16[256,512]{1,0:T(8,128)(2,1)} %param.13) | data formatting | bytes 524288 | tf_op args[4]
  12.3 1.9 %collective-permute-start.3 = (bf16[256,512]{0,1:T(8,128)(2,1)}, bf16[256,512]{0,1:T(8,128)(2,1)}, u32[]{:S(2)}, u32[]{:S(2)}) collective-permute-start(bf16[256,512]{0,1:T(8,128)(2,1)} %copy.14), channel_id=1, source_target_pairs={{510,0},{0,2},{2,4},{4,6},{6,8},{8,10},{10,12},{12,14},{14,16},{16... | collective-permute-start | bytes 786440 | tf_op jit(solution)/shard_map/ppermute | solution.py:205
  14.3 0.6 copy-done.14
  15.0 0.7 compare_convert_fusion.pick
  15.7 2.2 %all-gather.1 = f32[512,128]{1,0:T(8,128)} all-gather(f32[256,128]{1,0:T(8,128)S(1)} %pad_maximum_fusion), channel_id=3, replica_groups=mesh['top'=16,'b3'=2,'b2'=2,'b1'=2,'b0'=2,'blk'=2] {'blk'}, dimensions={0}, use_global_device_ids=true | all-gather | bytes 393216 | tf_op jit(solution)/shard_map/all_gather | solution.py:211
  18.0 4.4 %factor_body.1 = (f32[256,256]{1,0:T(8,128)}, f32[256,256]{1,0:T(8,128)}) custom-call(f32[2,256,128]{2,1,0:T(8,128)} %bitcast.39), custom_call_target="tpu_custom_call" | custom-call | tf_op jit(solution)/shard_map/factor_body/pallas_call | solution.py:188
  22.7 0.4 fusion.6
  23.1 0.5 copy-done.10
  23.6 0.3 convolution_add_fusion.2
  23.9 0.7 constant_dynamic-slice_fusion
  24.7 2.2 %all-gather = f32[512,256]{1,0:T(8,128)S(1)} all-gather(f32[256,256]{1,0:T(8,128)S(1)} %get-tuple-element.15), channel_id=2, replica_groups=mesh['top'=16,'b3'=2,'b2'=2,'b1'=2,'b0'=2,'blk'=2] {'blk'}, dimensions={0}, use_global_device_ids=true | all-gather | bytes 786432 | tf_op jit(solution)/shard_map/all_gather | solution.py:211
  26.9 0.7 dynamic-slice_bitcast_fusion.others
  27.6 2.9 %solve_body.1 = bf16[256,256]{1,0:T(8,128)(2,1)} custom-call(f32[256,256]{1,0:T(8,128)} %get-tuple-element.16.own, f32[256,256]{1,0:T(8,128)} %dynamic-slice_bitcast_fusion.others, f32[256,256]{1,0:T(8,128)} %get-tuple-element.9.inverse, f32[256,256]{1,0:T(8,128)} %get-tuple-element.10.transposed), custom_call_target="tpu_custom_call" | custom-call | tf_op jit(solution)/shard_map/solve_body/pallas_call | solution.py:188
  30.5 1.9 %collective-permute-start.4 = (bf16[256,256]{1,0:T(8,128)(2,1)}, bf16[256,256]{1,0:T(8,128)(2,1)S(1)}, u32[]{:S(2)}, u32[]{:S(2)}) collective-permute-start(bf16[256,256]{1,0:T(8,128)(2,1)} %solve_body.1), channel_id=1, source_target_pairs={{510,0},{0,2},{2,4},{4,6},{6,8},{8,10},{10,12},{12,14},{14,16},{16... | collective-permute-start | bytes 393224 | tf_op jit(solution)/shard_map/ppermute | solution.py:205
  32.4 2.1 %collective-permute-start.2 = (bf16[512,512]{1,0:T(8,128)(2,1)S(1)}, bf16[512,512]{1,0:T(8,128)(2,1)S(1)}, u32[]{:S(2)}, u32[]{:S(2)}) collective-permute-start(bf16[512,512]{1,0:T(8,128)(2,1)S(1)} %collective-permute-done.1), channel_id=1, source_target_pairs={{0,1},{1,0},{2,3},{3,2},{4,5},{5,4},{6,7},{7,6},{8,9},{9,8},{10,11... | collective-permute-start | bytes 1572872 | tf_op jit(solution)/shard_map/ppermute | solution.py:208
  34.6 2.2 %all-gather.2 = bf16[512,256]{1,0:T(8,128)(2,1)S(1)} all-gather(bf16[256,256]{1,0:T(8,128)(2,1)} %solve_body.1), channel_id=4, replica_groups=mesh['top'=16,'b3'=2,'b2'=2,'b1'=2,'b0'=2,'blk'=2] {'blk'}, dimensions={0}, use_global_device_ids=true | all-gather | bytes 393216 | tf_op jit(solution)/shard_map/all_gather | solution.py:211
  36.8 1.5 %fusion.3 = f32[512,512]{1,0:T(8,128)S(1)} fusion(bf16[512,512]{1,0:T(8,128)(2,1)S(1)} %collective-permute-done.1, bf16[512,1024]{1,0:T(8,128)(2,1)} %param.11, s32[]{:T(128)S(6)} %select_n.18), kind=kOutput, calls=%fused_computation.12 | convolution fusion | flops 268435456 | bytes 2097156 | tf_op jit(solution)/shard_map/dot_general | solution.py:17
  38.2 1.5 %convolution_add_fusion.1 = f32[512,512]{1,0:T(8,128)S(1)} fusion(f32[512,512]{1,0:T(8,128)S(1)} %fusion.6, bf16[512,512]{1,0:T(8,128)(2,1)} %collective-permute-done, bf16[512,1024]{1,0:T(8,128)(2,1)S(1)} %copy-done, s32[]{:T(128)S(6)} %select_n.19), kind=kOutput, calls=%fused_computation.3 | convolution fusion | flops 268697600 | bytes 3145732 | tf_op jit(solution)/shard_map/dot_general | solution.py:17
  40.3 5.0 %collective-permute-done.4 = bf16[256,256]{1,0:T(8,128)(2,1)S(1)} collective-permute-done((bf16[256,256]{1,0:T(8,128)(2,1)}, bf16[256,256]{1,0:T(8,128)(2,1)S(1)}, u32[]{:S(2)}, u32[]{:S(2)}) %collective-permute-start.4) | collective-permute-done | bytes 131104 | tf_op jit(solution)/shard_map/ppermute | solution.py:205
  45.3 2.1 %all-gather.3 = bf16[512,256]{1,0:T(8,128)(2,1)} all-gather(bf16[256,256]{1,0:T(8,128)(2,1)S(1)} %collective-permute-done.4), channel_id=5, replica_groups=mesh['top'=16,'b3'=2,'b2'=2,'b1'=2,'b0'=2,'blk'=2] {'blk'}, dimensions={0}, use_global_device_ids=true | all-gather | bytes 393216 | tf_op jit(solution)/shard_map/all_gather | solution.py:211
  47.4 1.4 %fusion.1.direct = f32[512,512]{1,0:T(8,128)} fusion(f32[512,512]{1,0:T(8,128)S(1)} %convolution_add_fusion.1, f32[512,512]{1,0:T(8,128)S(1)} %fusion.3, bf16[512,512]{1,0:T(8,128)(2,1)S(1)} %collective-permute-done.2, f32[512,256]{1,0:T(8,128)S(1)} %convolution_bitcast_fusion, f32[512,256]{1,0:T(8,128)S(1)} %convolution_bitcast_fusion.1, ...), kind=kOutput, calls=%fused_computation.2 | convolution fusion | flops 269484032 | bytes 5242884 | tf_op jit(solution)/shard_map/dot_general | solution.py:17
  48.8 2.9 %samples_body.1 = (f32[512,512]{1,0:T(8,128)}, bf16[256,512]{1,0:T(8,128)(2,1)}) custom-call(f32[512,512]{1,0:T(8,128)} %fusion.1.direct, bf16[512,256]{1,0:T(8,128)(2,1)} %bitcast.5.link, bf16[2,256,256]{2,1,0:T(8,128)(2,1)} %bitcast.40, bf16[128,512]{1,0:T(8,128)(2,1)} %compare_convert_fusion.pick), custom_call_target="tpu_custom_call" | custom-call | tf_op jit(solution)/shard_map/samples_body/pallas_call | solution.py:188
  51.7 2.4 %all-gather.4 = bf16[512,512]{1,0:T(8,128)(2,1)S(1)} all-gather(bf16[256,512]{1,0:T(8,128)(2,1)} %get-tuple-element.12), channel_id=6, replica_groups=mesh['top'=16,'b3'=2,'b2'=2,'b1'=2,'b0'=2,'blk'=2] {'blk'}, dimensions={0}, use_global_device_ids=true | all-gather | bytes 786432 | tf_op jit(solution)/shard_map/all_gather | solution.py:211
  54.1 0.7 slice_add_fusion.leaf
  54.9 11.8 %all-gather.5 = bf16[1,256,512]{2,1,0:T(8,128)(2,1)S(1)} all-gather(bf16[1,128,512]{2,1,0:T(8,128)(2,1)S(1)} %slice.48), channel_id=7, replica_groups=mesh['top'=16,'b3'=2,'b2'=2,'b1'=2,'b0'=2,'blk'=2] {'b0'}, dimensions={1}, use_global_device_ids=true | all-gather | bytes 393216 | tf_op jit(solution)/shard_map/all_gather | solution.py:268
  66.9 7.1 %all_gather.53.refs_1_ = bf16[256,512]{1,0:T(8,128)(2,1)S(1)} all-gather(bf16[128,512]{1,0:T(8,128)(2,1)S(1)} %convolution_convert_fusion.3.refs_4_), channel_id=1, replica_groups=mesh['top'=16,'b3'=2,'b2'=2,'b1'=2,'b0'=2,'blk'=2] {'b1'}, dimensions={0}, use_global_device_ids=true | all-gather | bytes 393216 | tf_op jit(solution)/shard_map/all_gather | solution.py:268
  74.3 5.6 %all_gather.54.refs_2_ = bf16[256,512]{1,0:T(8,128)(2,1)S(1)} all-gather(bf16[128,512]{1,0:T(8,128)(2,1)S(1)} %convolution_convert_fusion.2.refs_5_), channel_id=1, replica_groups=mesh['top'=16,'b3'=2,'b2'=2,'b1'=2,'b0'=2,'blk'=2] {'b2'}, dimensions={0}, use_global_device_ids=true | all-gather | bytes 393216 | tf_op jit(solution)/shard_map/all_gather | solution.py:268
  80.2 7.5 %all_gather.55.refs_3_ = bf16[256,512]{1,0:T(8,128)(2,1)S(1)} all-gather(bf16[128,512]{1,0:T(8,128)(2,1)S(1)} %convolution_convert_fusion.1.refs_6_), channel_id=1, replica_groups=mesh['top'=16,'b3'=2,'b2'=2,'b1'=2,'b0'=2,'blk'=2] {'b3'}, dimensions={0}, use_global_device_ids=true | all-gather | bytes 393216 | tf_op jit(solution)/shard_map/all_gather | solution.py:268
  87.8 0.9 convolution_convert_fusion.refs_7_
  88.7 10.8 %interp_body.1 = (f32[512,128]{1,0:T(8,128)}, f32[1,4,256,128]{3,2,1,0:T(8,128)}) custom-call(f32[512,512]{1,0:T(8,128)} %get-tuple-element.6.samples, bf16[256,512]{1,0:T(8,128)(2,1)} %slice_add_fusion.leaf, bf16[256,512]{1,0:T(8,128)(2,1)} %bitcast.37, bf16[256,512]{1,0:T(8,128)(2,1)} %copy-done.3, bf16[256,512]{1,0:T(8,128)(2,1)} %copy-done.4, ...), custom_call_target="tpu_custom_call" | custom-call | tf_op jit(solution)/shard_map/interp_body/pallas_call | solution.py:188
  (45 shorter events, 1.7 us)
Async XLA Ops:
  0.6 22.0 %copy-start = (bf16[512,1024]{1,0:T(8,128)(2,1)S(1)}, bf16[512,1024]{1,0:T(8,128)(2,1)}, u32[]{:S(2)}) copy-start(bf16[512,1024]{1,0:T(8,128)(2,1)} %param.10) | copy-start | bytes 3145732
  0.6 14.3 %copy-start.12 = (f32[128,128]{1,0:T(8,128)S(1)}, f32[128,128]{1,0:T(8,128)}, u32[]{:S(2)}) copy-start(f32[128,128]{1,0:T(8,128)} %param.15) | copy-start | bytes 196612
  0.7 14.3 %copy-start.13 = (f32[128,128]{1,0:T(8,128)S(1)}, f32[128,128]{1,0:T(8,128)}, u32[]{:S(2)}) copy-start(f32[128,128]{1,0:T(8,128)} %param.14) | copy-start | bytes 196612
  0.7 37.6 %collective-permute-start = (bf16[512,512]{1,0:T(8,128)(2,1)}, bf16[512,512]{1,0:T(8,128)(2,1)}, u32[]{:S(2)}, u32[]{:S(2)}) collective-permute-start(bf16[512,512]{1,0:T(8,128)(2,1)} %param.9), channel_id=1, source_target_pairs={{0,1},{1,0},{2,3},{3,2},{4,5},{5,4},{6,7},{7,6},{8,9},{9,8},{10,11... | collective-permute-start | bytes 1572872 | tf_op jit(solution)/shard_map/ppermute | solution.py:208
  2.7 20.4 %collective-permute-start.1 = (bf16[512,512]{1,0:T(8,128)(2,1)}, bf16[512,512]{1,0:T(8,128)(2,1)S(1)}, u32[]{:S(2)}, u32[]{:S(2)}) collective-permute-start(bf16[512,512]{1,0:T(8,128)(2,1)} %param.9), channel_id=1, source_target_pairs={{2,0},{4,2},{6,4},{8,6},{10,8},{12,10},{14,12},{16,14},{18,16},{20... | collective-permute-start | bytes 1572872 | tf_op jit(solution)/shard_map/ppermute | solution.py:205
  12.3 36.5 %collective-permute-start.3 = (bf16[256,512]{0,1:T(8,128)(2,1)}, bf16[256,512]{0,1:T(8,128)(2,1)}, u32[]{:S(2)}, u32[]{:S(2)}) collective-permute-start(bf16[256,512]{0,1:T(8,128)(2,1)} %copy.14), channel_id=1, source_target_pairs={{510,0},{0,2},{2,4},{4,6},{6,8},{8,10},{10,12},{12,14},{14,16},{16... | collective-permute-start | bytes 786440 | tf_op jit(solution)/shard_map/ppermute | solution.py:205
  14.2 0.7 copy-start.14
  14.2 0.7 copy-start.15
  14.9 7.4 %copy-start.6 = (bf16[512,512]{1,0:T(8,128)(2,1)S(1)}, bf16[512,512]{1,0:T(8,128)(2,1)}, u32[]{:S(2)}) copy-start(bf16[512,512]{1,0:T(8,128)(2,1)} %param.9) | copy-start | bytes 1572868
  15.7 6.7 %copy-start.1 = (bf16[256,512]{1,0:T(8,128)(2,1)S(1)}, bf16[256,512]{1,0:T(8,128)(2,1)}, u32[]{:S(2)}) copy-start(bf16[256,512]{1,0:T(8,128)(2,1)} %param.12) | copy-start | bytes 786436
  22.7 1.0 copy-start.10
  30.5 14.8 %collective-permute-start.4 = (bf16[256,256]{1,0:T(8,128)(2,1)}, bf16[256,256]{1,0:T(8,128)(2,1)S(1)}, u32[]{:S(2)}, u32[]{:S(2)}) collective-permute-start(bf16[256,256]{1,0:T(8,128)(2,1)} %solve_body.1), channel_id=1, source_target_pairs={{510,0},{0,2},{2,4},{4,6},{6,8},{8,10},{10,12},{12,14},{14,16},{16... | collective-permute-start | bytes 393224 | tf_op jit(solution)/shard_map/ppermute | solution.py:205
  32.4 15.0 %collective-permute-start.2 = (bf16[512,512]{1,0:T(8,128)(2,1)S(1)}, bf16[512,512]{1,0:T(8,128)(2,1)S(1)}, u32[]{:S(2)}, u32[]{:S(2)}) collective-permute-start(bf16[512,512]{1,0:T(8,128)(2,1)S(1)} %collective-permute-done.1), channel_id=1, source_target_pairs={{0,1},{1,0},{2,3},{3,2},{4,5},{5,4},{6,7},{7,6},{8,9},{9,8},{10,11... | collective-permute-start | bytes 1572872 | tf_op jit(solution)/shard_map/ppermute | solution.py:208
  39.7 7.7 %copy-start.11 = (bf16[512,1024]{1,0:T(8,128)(2,1)S(1)}, bf16[512,1024]{1,0:T(8,128)(2,1)}, u32[]{:S(2)}) copy-start(bf16[512,1024]{1,0:T(8,128)(2,1)} %param.11) | copy-start | bytes 3145732
  66.7 7.4 %copy-start.2 = (bf16[1,256,512]{2,1,0:T(8,128)(2,1)}, bf16[1,256,512]{2,1,0:T(8,128)(2,1)S(1)}, u32[]{:S(2)}) copy-start(bf16[1,256,512]{2,1,0:T(8,128)(2,1)S(1)} %all-gather.5) | copy-start | bytes 786436
  66.9 7.2 %copy-start.7 = (bf16[128,512]{1,0:T(8,128)(2,1)}, bf16[128,512]{1,0:T(8,128)(2,1)S(1)}, u32[]{:S(2)}) copy-start(bf16[128,512]{1,0:T(8,128)(2,1)S(1)} %convolution_convert_fusion.3.refs_4_) | copy-start | bytes 393220
  74.1 5.9 %copy-start.3 = (bf16[256,512]{1,0:T(8,128)(2,1)}, bf16[256,512]{1,0:T(8,128)(2,1)S(1)}, u32[]{:S(2)}) copy-start(bf16[256,512]{1,0:T(8,128)(2,1)S(1)} %all_gather.53.refs_1_) | copy-start | bytes 786436
  74.3 5.7 %copy-start.8 = (bf16[128,512]{1,0:T(8,128)(2,1)}, bf16[128,512]{1,0:T(8,128)(2,1)S(1)}, u32[]{:S(2)}) copy-start(bf16[128,512]{1,0:T(8,128)(2,1)S(1)} %convolution_convert_fusion.2.refs_5_) | copy-start | bytes 393220
  80.0 7.8 %copy-start.4 = (bf16[256,512]{1,0:T(8,128)(2,1)}, bf16[256,512]{1,0:T(8,128)(2,1)S(1)}, u32[]{:S(2)}) copy-start(bf16[256,512]{1,0:T(8,128)(2,1)S(1)} %all_gather.54.refs_2_) | copy-start | bytes 786436
  80.2 7.6 %copy-start.9 = (bf16[128,512]{1,0:T(8,128)(2,1)}, bf16[128,512]{1,0:T(8,128)(2,1)S(1)}, u32[]{:S(2)}) copy-start(bf16[128,512]{1,0:T(8,128)(2,1)S(1)} %convolution_convert_fusion.1.refs_6_) | copy-start | bytes 393220
  87.8 0.9 copy-start.5
where the time goes:
time: 100 us; the launch traced here: 99.5 us
  blocking collectives  43.3 us (43%)
  Pallas kernels  21 us (21%)
  starting transfers between devices  15.8 us (16%)
  matrix products  7.55 us (8%)
  waiting for transfers between devices  4.98 us (5%)
  local copies, waits for them, and re-layouts  4.48 us (4%)
  other arithmetic  1.52 us (2%)
    all_gather x4, blocking collectives, per_device(): pair = lax.all_gather(chosen, axis, axis=0, tiled=True)  32.2 us
    pallas_call x4, Pallas kernels, call(): pl.pallas_call(body, out_shape=shapes if len(shapes) > 1 else shapes[0],...  21 us
    ppermute x3, starting transfers between devices, shifted(): return lax.ppermute(block, leaf, route)  11.6 us
    all_gather x5, blocking collectives, both(): return lax.all_gather(block, 'blk', axis=0)  11.1 us
    dot_general x12, matrix products, dot1(): return lax.dot_general(a, b, dims, preferred_element_type=f32)  7.55 us
    ppermute x3, waiting for transfers between devices, shifted(): return lax.ppermute(block, leaf, route)  4.98 us
    ppermute x2, starting transfers between devices, swapped(): return lax.ppermute(block, 'blk', [(0, 1), (1, 0)])  4.18 us
    unnamed x33, local copies, waits for them, and re-layouts  3 us
  transfers between devices with their start and end apart: 5, of which 1 were waited for; matrix products, arithmetic and copies ran while one was open for 10% of the time, Pallas kernels for 7%

commit v1 on v0

v1 whole, which is shorter than its diff:
```python
import jax
import jax.numpy as jnp
from jax import lax
from jax.experimental import pallas as pl
from jax.experimental.pallas import tpu as pltpu
from jax.sharding import Mesh, PartitionSpec as P

f32 = jnp.float32
bf16 = jnp.bfloat16
highest = lax.Precision.HIGHEST
STEP = 16
BITS = ("b3", "b2", "b1", "b0")
NN = (((1,), (0,)), ((), ()))
NT = (((1,), (1,)), ((), ()))


def dot1(a, b, dims=NN):
    return lax.dot_general(a, b, dims, preferred_element_type=f32)


def dot6(a, b, dims=NN):
    return lax.dot_general(a, b, dims, preferred_element_type=f32, precision=highest)


def halves(a):
    high = a.astype(bf16)
    return high, (a - high.astype(f32)).astype(bf16)


def dot3(a, b, dims=NN):
    (ah, al), (bh, bl) = halves(a), halves(b)
    return dot1(ah, bh, dims) + (dot1(ah, bl, dims) + dot1(al, bh, dims))


def iota(shape, dim):
    return lax.broadcasted_iota(jnp.int32, shape, dim)


def lane_columns(packed):
    first = iota(packed.shape, 1) // STEP * STEP
    return [
        jnp.take_along_axis(packed, first + j, axis=1, mode="promise_in_bounds")
        for j in range(STEP)
    ]


def lane_packed(columns):
    at = iota(columns[0].shape, 1) % STEP
    parts = [jnp.where(at == j, c, 0.0) for j, c in enumerate(columns)]
    while len(parts) > 1:
        parts = [a + b for a, b in zip(parts[::2], parts[1::2])]
    return parts[0]


def group_inverse(packed):
    tile = (8, packed.shape[1])
    parts = range(STEP // 8)
    columns = list(zip(*(lane_columns(packed[p * 8 : p * 8 + 8]) for p in parts)))
    row = iota(tile, 0)
    scale = [jnp.ones(tile, f32) for _ in parts]
    for k in range(STEP):
        at, here = k // 8, row == k % 8
        spread = [jnp.broadcast_to(c[at][k % 8 : k % 8 + 1], tile) for c in columns]
        inv = 1.0 / spread[k]
        scale[at] = jnp.where(here, inv, scale[at])
        multiple = [columns[k][p] * inv for p in parts]
        multiple[at] = jnp.where(here, 0.0, multiple[at])
        pivot = [-m for m in multiple]
        pivot[at] = jnp.where(here, 1.0, pivot[at])
        columns = [
            pivot if j == k else [c[p] - multiple[p] * spread[j] for p in parts]
            for j, c in enumerate(columns)
        ]
    return jnp.concatenate([lane_packed([c[p] * scale[p] for c in columns]) for p in parts], axis=0)


def group_lower_inverse(packed):
    columns = lane_columns(packed)
    row = iota(packed.shape, 0)
    x = jnp.where(row == iota(packed.shape, 1) % STEP, 1.0, 0.0)
    for k in range(STEP):
        pivot = x[k : k + 1] / columns[k][k : k + 1]
        below = jnp.where(row > k, columns[k], 0.0)
        x = jnp.where(row == k, pivot, x - below * pivot)
    return x


def block_rows(packed):
    size = packed.shape[1]
    same = iota((size, size), 0) // STEP == iota((size, size), 1) // STEP
    return jnp.where(same, jnp.concatenate([packed] * (size // STEP), axis=0), 0.0)


def lower_inverse(lower):
    size = lower.shape[0]
    group = iota((STEP, size), 1) // STEP
    packed = jnp.zeros((STEP, size), f32)
    for q in range(size // STEP):
        packed = jnp.where(group == q, lower[q * STEP : (q + 1) * STEP], packed)
    x = block_rows(group_lower_inverse(packed))
    row, col = iota((size, size), 0), iota((size, size), 1)
    width = STEP
    while width < size:
        pair = (row // width == col // width + 1) & (col // width % 2 == 0)
        x = x - dot6(x, dot6(jnp.where(pair, lower, 0.0), x))
        width *= 2
    return x


def picks(listed, count, first):
    rank = listed.shape[1]
    wanted = jnp.broadcast_to(listed, (rank, rank)).T
    place = iota((rank, rank), 1) + first
    return jnp.concatenate(
        [jnp.where(wanted == place + c, 1.0, 0.0).astype(bf16) for c in range(0, count, rank)], axis=1
    )


def factor_body(blocks, link, sketch, leaf_set, merge_sets, inverse, transposed, base, leaf_pick, merge_pick):
    base[...] = dot1(link[...], sketch[...])
    size = blocks.shape[2]
    low = iota((size, size), 0) >= iota((size, size), 1)
    first = lower_inverse(jnp.where(low, blocks[0, :size], 0.0))
    last = lower_inverse(jnp.where(low, blocks[1, :size], 0.0))
    corner = -dot6(last, dot6(blocks[1, size:], first))
    whole = jnp.concatenate(
        [
            jnp.concatenate([first, jnp.zeros((size, size), f32)], axis=1),
            jnp.concatenate([corner, last], axis=1),
        ],
        axis=0,
    )
    inverse[0], inverse[1] = halves(whole)
    transposed[0], transposed[1] = halves(whole.T)
    rows = leaf_pick.shape[1]
    leaf_pick[...] = picks(leaf_set[...], rows, lax.axis_index("blk") * rows)
    for j in range(merge_pick.shape[0]):
        merge_pick[j] = picks(merge_sets[0, j : j + 1], merge_pick.shape[2], 0)


def load_body(base, link, sketch, kept, sent):
    here = lax.axis_index("blk")
    width = kept.shape[1]
    for out, half in ((kept, here), (sent, 1 - here)):
        at = pl.ds(pl.multiple_of(half * width, width), width)
        out[...] = base[:, at] + dot1(link[...], sketch[:, at])


def split_dot(left, right):
    high, low = halves(right)
    return dot1(left[0], high) + (dot1(left[0], low) + dot1(left[1], high))


def solve_body(kept, got, inverse, transposed, weights):
    load = kept[...] + got[1 - lax.axis_index("blk")]
    weights[...] = split_dot(transposed, split_dot(inverse, load)).astype(bf16)


def carry_body(weights, previous, pick, packed):
    rows = weights.shape[0]
    packed[:rows] = weights[...]
    packed[rows:] = dot1(pick[...], previous[...], NT).astype(bf16)


def direct_body(
    near, following, own, other, next_own, next_other, link, previous, carried, pick, direct, turned_link, pre, link_rows
):
    here = lax.axis_index("blk")
    rows = own.shape[0]
    mine = pl.ds(pl.multiple_of(here * rows, rows), rows)
    theirs = pl.ds(pl.multiple_of((1 - here) * rows, rows), rows)
    inner, width, count = link.shape[0], carried.shape[2], pick.shape[0]
    link_rows[...] = carried[0, inner:] + carried[1, inner:]
    turned_link[...] = previous[...].T
    back = link[...].T
    for c in range(carried.shape[0]):
        at = slice(c * width, (c + 1) * width)
        part = (
            dot1(near[:, mine], own[:, at])
            + dot1(near[:, theirs], other[:, at])
            + dot1(following[:, mine], next_own[:, at])
            + dot1(following[:, theirs], next_other[:, at])
            - dot1(back, carried[c, :inner])
        )
        direct[:, at] = part
        high, low = halves(part)
        pre[:count, at] = dot1(pick[...], high).astype(bf16)
        pre[count:, at] = dot1(pick[...], low).astype(bf16)


def summed(pieces, count, at):
    return sum(pieces[c, r : r + count, at].astype(f32) for c in range(2) for r in (0, count))


def chosen_body(pieces, link_rows, weights, chosen):
    here = lax.axis_index("blk")
    count, width = chosen.shape
    at = pl.ds(pl.multiple_of(here * width, width), width)
    chosen[...] = (summed(pieces, count, at) - dot1(link_rows[...], weights[...])).astype(bf16)


def pack_body(weights, *refs):
    pairs, packed = refs[:-1], refs[-1]
    rank = pairs[0].shape[0] // 2
    for j, pair in enumerate(pairs):
        other = 1 - lax.axis_index(BITS[-1 - j])
        packed[j * rank : (j + 1) * rank] = pair[pl.ds(pl.multiple_of(other * rank, rank), rank), :]
    packed[len(pairs) * rank :] = weights[...]


def turned(rows, by):
    return jnp.concatenate([rows[rows.shape[0] - by :], rows[: rows.shape[0] - by]], axis=0) if by else rows


def invert_all(gram, count, size, beside):
    groups = size // STEP
    group = iota((STEP, size), 1) // STEP
    wide_group = iota((size, size), 1) // STEP
    same = iota((size, size), 0) // STEP == wide_group
    unit = jnp.where(iota((STEP, size), 0) == iota((STEP, size), 1) % STEP, 1.0, 0.0)
    panels = [gram[g, :STEP, :] for g in range(count)]
    for k in range(groups):
        rows = slice(k * STEP, (k + 1) * STEP)
        places = [(k + g) % groups for g in range(count)]
        packed = unit
        for g, q in enumerate(places):
            packed = jnp.where(group == q, panels[g], packed)
        pivots = block_rows(group_inverse(packed))
        if k < len(beside):
            beside[k]()
        stacked = [jnp.zeros((STEP, size), f32)] * groups
        for g, q in enumerate(places):
            stacked[q] = panels[g]
        scaled = dot3(pivots, jnp.concatenate(stacked, axis=0))
        scaled = jnp.where(same, pivots, scaled)
        if k + 1 < groups:
            below = slice((k + 1) * STEP, (k + 2) * STEP)
            ahead = [gram[g, below, :] for g in range(count)]
            left = [jnp.where(group == q, a, 0.0) for q, a in zip(places, ahead)]
            change = dot3(jnp.concatenate(left, axis=0), scaled)
            panels = [
                jnp.where(group == q, 0.0, a) - change[g * STEP : (g + 1) * STEP]
                for g, (q, a) in enumerate(zip(places, ahead))
            ]
        left = [jnp.where(wide_group == q, gram[g], 0.0) for g, q in enumerate(places)]
        change = dot3(jnp.concatenate(left, axis=0), scaled)
        for g, q in enumerate(places):
            gram[g] = jnp.where(wide_group == q, 0.0, gram[g]) - change[g * size : (g + 1) * size]
            gram[g, rows, :] = scaled[q * STEP : (q + 1) * STEP]


def interp_body(
    direct, turned_link, pieces, link_rows, gathered, picks_of,
    samples_out, leaf_interp, merge_interp, samples, gram, cross, candidates, sent,
):
    levels, rank = picks_of.shape[0], gram.shape[1]
    width = gathered.shape[2]
    own = slice(levels * rank, gathered.shape[1])
    high, low = zip(*(
        halves(
            summed(pieces, rank, slice(c * width, (c + 1) * width))
            - dot1(link_rows[...], gathered[c, own])
        )
        for c in range(2)
    ))
    high, low = jnp.concatenate(high, axis=1), jnp.concatenate(low, axis=1)
    picked = []
    for j in range(levels):
        mine = picked[-1] if picked else high
        sibling = jnp.concatenate([gathered[c, j * rank : (j + 1) * rank] for c in range(2)], axis=1)
        upper = lax.axis_index(BITS[-1 - j])
        candidates[j, pl.ds(pl.multiple_of(upper * rank, rank), rank), :] = mine
        candidates[j, pl.ds(pl.multiple_of((1 - upper) * rank, rank), rank), :] = sibling
        picked.append(dot1(picks_of[j], candidates[j]).astype(bf16))
    spun = [turned(rows, STEP * (j + 1)) for j, rows in enumerate(picked)]
    gram[0] = dot1(high, high, NT) + (dot1(high, low, NT) + dot1(low, high, NT))
    for j in range(levels):
        gram[j + 1] = dot1(picked[j], spun[j], NT)
    tall = leaf_interp.shape[0]
    wide = merge_interp.shape[2]

    def finish():
        for c in range(2):
            at = slice(c * width, (c + 1) * width)
            samples[:, at] = (
                direct[:, at]
                - dot1(turned_link[...], gathered[c, own])
            )
        writing.start()

    def leaf_cross():
        yh, yl = halves(samples[...])
        cross[:tall] = dot1(yh, high, NT) + (dot1(yh, low, NT) + dot1(yl, high, NT))

    def merge_cross(j):
        cross[tall + j * wide : tall + (j + 1) * wide] = dot1(candidates[j], spun[j], NT)

    writing = pltpu.make_async_copy(samples, samples_out, sent)
    beside = [finish, leaf_cross] + [lambda j=j: merge_cross(j) for j in range(levels)]
    invert_all(gram, levels + 1, rank, beside)
    leaf_interp[...] = dot3(cross[:tall], gram[0], NT)
    for j in range(levels):
        merge_interp[0, j] = dot3(cross[tall + j * wide : tall + (j + 1) * wide], gram[j + 1], NT)
    writing.wait()


def call(body, outs, *args, scratch=(), far=0):
    shapes = tuple(jax.ShapeDtypeStruct(s, t) for s, t in outs)
    places = [pl.BlockSpec(memory_space=pl.ANY if i < far else pltpu.VMEM) for i in range(len(outs))]
    return pl.pallas_call(
        body,
        out_shape=shapes if len(shapes) > 1 else shapes[0],
        out_specs=tuple(places) if len(shapes) > 1 else places[0],
        scratch_shapes=list(scratch),
        compiler_params=pltpu.CompilerParams(vmem_limit_bytes=16 << 20),
    )(*args)


def solution(mesh):
    leaf_count, blk_count = mesh.shape["leaf"], mesh.shape["blk"]
    names = ("top", *BITS, "blk")
    fine = Mesh(mesh.devices.reshape(leaf_count >> 4, 2, 2, 2, 2, blk_count), names)
    leaf = names[:-1]

    def shifted(block, distance):
        route = [((i - distance) % leaf_count, i) for i in range(leaf_count)]
        return lax.ppermute(block, leaf, route)

    def swapped(block):
        return lax.ppermute(block, "blk", [(0, 1), (1, 0)])

    def both(block):
        return lax.all_gather(block, "blk", axis=0)

    def per_device(
        sketch, near_block, next_block, link_own, link_next, diag_block, sub_block, leaf_set, merge_sets
    ):
        rows, cols = sketch.shape
        interior = link_own.shape[0]
        rank = leaf_set.shape[1]
        half = cols // 2

        levels = merge_sets.shape[1]
        next_half = shifted(sketch, -1)
        other_half = swapped(sketch)
        previous_link = shifted(link_next, 1)
        factors = both(jnp.concatenate([diag_block, sub_block], axis=0))
        inverse, transposed, base, leaf_pick, merge_pick = call(
            factor_body,
            [
                ((2, interior, interior), bf16),
                ((2, interior, interior), bf16),
                ((interior, cols), f32),
                ((rank, rows), bf16),
                ((levels, rank, 2 * rank), bf16),
            ],
            factors,
            link_own,
            sketch,
            leaf_set,
            merge_sets,
        )
        kept, sent = call(load_body, [((interior, half), f32)] * 2, base, link_next, next_half)
        weights = call(solve_body, [((interior, half), bf16)], kept, both(sent), inverse, transposed)
        previous_weights = shifted(weights, 1)
        next_other = swapped(next_half)
        packed = call(
            carry_body, [((interior + rank, half), bf16)], weights, previous_link, leaf_pick
        )
        direct, turned_link, pre, link_rows = call(
            direct_body,
            [((rows, cols), f32), ((rows, interior), bf16), ((2 * rank, cols), bf16), ((rank, interior), bf16)],
            near_block,
            next_block,
            sketch,
            other_half,
            next_half,
            next_other,
            link_own,
            previous_link,
            both(packed),
            leaf_pick,
        )
        pieces = both(pre)
        chosen = call(chosen_body, [((rank, half), bf16)], pieces, link_rows, previous_weights)
        pairs = []
        for level, axis in enumerate(reversed(BITS)):
            pairs.append(lax.all_gather(chosen, axis, axis=0, tiled=True))
            if level + 1 < levels:
                chosen = dot1(merge_pick[level], pairs[-1]).astype(bf16)
        gathered = both(
            call(pack_body, [((levels * rank + interior, half), bf16)], previous_weights, *pairs)
        )
        samples, leaf_interp, merge_interp = call(
            interp_body,
            [((rows, cols), f32), ((rows, rank), f32), ((1, levels, 2 * rank, rank), f32)],
            direct,
            turned_link,
            pieces,
            link_rows,
            gathered,
            merge_pick,
            scratch=[
                pltpu.VMEM((rows, cols), f32),
                pltpu.VMEM((levels + 1, rank, rank), f32),
                pltpu.VMEM((rows + levels * 2 * rank, rank), f32),
                pltpu.VMEM((levels, 2 * rank, cols), bf16),
                pltpu.SemaphoreType.DMA,
            ],
            far=1,
        )
        return samples, leaf_interp, merge_interp

    split = P((*leaf, "blk"), None)
    linked = P(leaf, "blk")
    return jax.shard_map(
        per_device,
        mesh=fine,
        in_specs=(split, split, split, linked, linked, split, split, P(leaf, None), P(leaf, None, None)),
        out_specs=(split, split, P((*leaf, "blk"), None, None, None)),
        check_vma=False,
    )
```

time: 100 us -> 91.9 us (0.919)
  the two profiles are of different devices: /device:TPU:2 before, /device:TPU:1 now
where the time goes in v1:
time: 91.9 us; the launch traced here: 91.4 us
  blocking collectives  33.8 us (37%)
  starting transfers between devices  26.8 us (29%)
  Pallas kernels  15.4 us (17%)
  waiting for transfers between devices  11.6 us (13%)
  local copies, waits for them, and re-layouts  1.63 us (2%)
    ppermute x3, starting transfers between devices, shifted(): return lax.ppermute(block, leaf, route)  20.6 us
    all_gather x4, blocking collectives, per_device(): pairs.append(lax.all_gather(chosen, axis, axis=0, tiled=True))  17.9 us
    all_gather x5, blocking collectives, both(): return lax.all_gather(block, 'blk', axis=0)  15.8 us
    pallas_call x8, Pallas kernels, call(): pl.pallas_call(body, out_shape=shapes if len(shapes) > 1 else shapes[0],...  15.4 us
    ppermute x3, waiting for transfers between devices, shifted(): return lax.ppermute(block, leaf, route)  11.6 us
    ppermute x2, starting transfers between devices, swapped(): return lax.ppermute(block, 'blk', [(0, 1), (1, 0)])  6.29 us
  transfers between devices with their start and end apart: 5, of which 3 were waited for; matrix products, arithmetic and copies ran while one was open for 1% of the time, Pallas kernels for 7%

profile of v1, /device:TPU:1, one launch (start us, length us, event | category | flops | bytes accessed | tf_op | source)
XLA Modules:
  0.0 91.4 jit_solution(17743192639171977149)
XLA Ops:
  0.6 16.7 %collective-permute-start.1 = (bf16[512,512]{1,0:T(8,128)(2,1)}, bf16[512,512]{1,0:T(8,128)(2,1)S(1)}, u32[]{:S(2)}, u32[]{:S(2)}) collective-permute-start(bf16[512,512]{1,0:T(8,128)(2,1)} %own.1), channel_id=1, source_target_pairs={{2,0},{4,2},{6,4},{8,6},{10,8},{12,10},{14,12},{16,14},{18,16},{20... | collective-permute-start | bytes 1572872 | tf_op jit(solution)/shard_map/ppermute | solution.py:327
  17.4 2.9 %collective-permute-start = (bf16[512,512]{1,0:T(8,128)(2,1)}, bf16[512,512]{1,0:T(8,128)(2,1)S(1)}, u32[]{:S(2)}, u32[]{:S(2)}) collective-permute-start(bf16[512,512]{1,0:T(8,128)(2,1)} %own.1), channel_id=1, source_target_pairs={{0,1},{1,0},{2,3},{3,2},{4,5},{5,4},{6,7},{7,6},{8,9},{9,8},{10,11... | collective-permute-start | bytes 1572872 | tf_op jit(solution)/shard_map/ppermute | solution.py:330
  20.2 8.0 %collective-permute-done.1.sketch.next_own = bf16[512,512]{1,0:T(8,128)(2,1)S(1)} collective-permute-done((bf16[512,512]{1,0:T(8,128)(2,1)}, bf16[512,512]{1,0:T(8,128)(2,1)S(1)}, u32[]{:S(2)}, u32[]{:S(2)}) %collective-permute-start.1) | collective-permute-done | bytes 524320 | tf_op jit(solution)/shard_map/ppermute | solution.py:327
  28.3 3.4 %collective-permute-start.2 = (bf16[512,512]{1,0:T(8,128)(2,1)S(1)}, bf16[512,512]{1,0:T(8,128)(2,1)S(1)}, u32[]{:S(2)}, u32[]{:S(2)}) collective-permute-start(bf16[512,512]{1,0:T(8,128)(2,1)S(1)} %collective-permute-done.1.sketch.next_own), channel_id=1, source_target_pairs={{0,1},{1,0},{2,3},{3,2},{4,5},{5,4},{6,7},{7,6},{8,9},{9,8},{10,11... | collective-permute-start | bytes 1572872 | tf_op jit(solution)/shard_map/ppermute | solution.py:330
  31.7 1.9 %collective-permute-start.3 = (bf16[256,512]{1,0:T(8,128)(2,1)}, bf16[256,512]{1,0:T(8,128)(2,1)S(1)}, u32[]{:S(2)}, u32[]{:S(2)}) collective-permute-start(bf16[256,512]{1,0:T(8,128)(2,1)} %link.4), channel_id=1, source_target_pairs={{510,0},{0,2},{2,4},{4,6},{6,8},{8,10},{10,12},{12,14},{14,16},{16... | collective-permute-start | bytes 786440 | tf_op jit(solution)/shard_map/ppermute | solution.py:327
  33.6 0.9 pad_maximum_fusion
  34.5 0.0 copy-start.6
  34.5 2.0 %all-gather = f32[512,128]{1,0:T(8,128)S(1)} all-gather(f32[256,128]{1,0:T(8,128)S(1)} %pad_maximum_fusion), channel_id=2, replica_groups=mesh['top'=16,'b3'=2,'b2'=2,'b1'=2,'b0'=2,'blk'=2] {'blk'}, dimensions={0}, use_global_device_ids=true | all-gather | bytes 393216 | tf_op jit(solution)/shard_map/all_gather | solution.py:333
  36.5 0.6 copy-done.7
  37.2 0.9 %copy-done.3 = bf16[256,512]{1,0:T(8,128)(2,1)S(1)} copy-done((bf16[256,512]{1,0:T(8,128)(2,1)S(1)}, bf16[256,512]{1,0:T(8,128)(2,1)}, u32[]{:S(2)}) %copy-start.3) | copy-done | bytes 262168
  38.1 2.8 %shard_map.112 = (bf16[2,256,256]{2,1,0:T(8,128)(2,1)S(1)}, bf16[2,256,256]{2,1,0:T(8,128)(2,1)S(1)}, f32[256,512]{1,0:T(8,128)S(1)}, bf16[128,512]{1,0:T(8,128)(2,1)S(1)}, bf16[4,128,256]{2,1,0:T(8,128)(2,1)S(1)}) custom-call(f32[2,256,128]{2,1,0:T(8,128)S(1)} %bitcast.22, bf16[256,512]{1,0:T(8,128)(2,1)S(1)} %copy-done.3, bf16[512,512]{1,0:T(8,128)(2,1)S(1)} %copy-done, ...), custom_call_target="tpu_custom_call" | custom-call | tf_op jit(solution)/shard_map/pallas_call | solution.py:310
  41.0 0.3 shard_map.113
  41.3 2.2 %all-gather.1 = f32[512,256]{1,0:T(8,128)S(1)} all-gather(f32[256,256]{1,0:T(8,128)S(1)} %get-tuple-element.16), channel_id=3, replica_groups=mesh['top'=16,'b3'=2,'b2'=2,'b1'=2,'b0'=2,'blk'=2] {'blk'}, dimensions={0}, use_global_device_ids=true | all-gather | bytes 786432 | tf_op jit(solution)/shard_map/all_gather | solution.py:333
  43.5 0.7 shard_map.114.weights
  44.2 1.9 %collective-permute-start.4 = (bf16[256,256]{1,0:T(8,128)(2,1)S(1)}, bf16[256,256]{1,0:T(8,128)(2,1)S(1)}, u32[]{:S(2)}, u32[]{:S(2)}) collective-permute-start(bf16[256,256]{1,0:T(8,128)(2,1)S(1)} %shard_map.114.weights), channel_id=1, source_target_pairs={{510,0},{0,2},{2,4},{4,6},{6,8},{8,10},{10,12},{12,14},{14,16},{16... | collective-permute-start | bytes 393224 | tf_op jit(solution)/shard_map/ppermute | solution.py:327
  46.1 1.9 %collective-permute-done.3.previous = bf16[256,512]{1,0:T(8,128)(2,1)S(1)} collective-permute-done((bf16[256,512]{1,0:T(8,128)(2,1)}, bf16[256,512]{1,0:T(8,128)(2,1)S(1)}, u32[]{:S(2)}, u32[]{:S(2)}) %collective-permute-start.3) | collective-permute-done | bytes 262176 | tf_op jit(solution)/shard_map/ppermute | solution.py:327
  48.0 0.2 shard_map.115
  48.2 0.0 copy-start.4
  48.2 2.4 %all-gather.2 = bf16[768,256]{1,0:T(8,128)(2,1)S(1)} all-gather(bf16[384,256]{1,0:T(8,128)(2,1)S(1)} %shard_map.115), channel_id=4, replica_groups=mesh['top'=16,'b3'=2,'b2'=2,'b1'=2,'b0'=2,'blk'=2] {'blk'}, dimensions={0}, use_global_device_ids=true | all-gather | bytes 589824 | tf_op jit(solution)/shard_map/all_gather | solution.py:333
  50.7 2.8 %shard_map.116 = (f32[512,512]{1,0:T(8,128)S(1)}, bf16[512,256]{1,0:T(8,128)(2,1)S(1)}, bf16[256,512]{1,0:T(8,128)(2,1)S(1)}, bf16[128,256]{1,0:T(8,128)(2,1)S(1)}) custom-call(bf16[512,1024]{1,0:T(8,128)(2,1)S(1)} %copy-done.1, bf16[512,1024]{1,0:T(8,128)(2,1)S(1)} %copy-done.2, bf16[512,512]{1,0:T(8,128)(2,1)S(1)} %copy-done, ...), custom_call_target="tpu_custom_call" | custom-call | tf_op jit(solution)/shard_map/pallas_call | solution.py:310
  53.5 2.2 %all-gather.3 = bf16[512,512]{1,0:T(8,128)(2,1)S(1)} all-gather(bf16[256,512]{1,0:T(8,128)(2,1)S(1)} %get-tuple-element.22), channel_id=5, replica_groups=mesh['top'=16,'b3'=2,'b2'=2,'b1'=2,'b0'=2,'blk'=2] {'blk'}, dimensions={0}, use_global_device_ids=true | all-gather | bytes 786432 | tf_op jit(solution)/shard_map/all_gather | solution.py:333
  55.7 1.7 %collective-permute-done.4.weights = bf16[256,256]{1,0:T(8,128)(2,1)S(1)} collective-permute-done((bf16[256,256]{1,0:T(8,128)(2,1)S(1)}, bf16[256,256]{1,0:T(8,128)(2,1)S(1)}, u32[]{:S(2)}, u32[]{:S(2)}) %collective-permute-start.4) | collective-permute-done | bytes 131104 | tf_op jit(solution)/shard_map/ppermute | solution.py:327
  57.3 0.2 shard_map.117
  57.5 3.8 %all_gather.50.refs_0_ = bf16[256,256]{1,0:T(8,128)(2,1)S(1)} all-gather(bf16[128,256]{1,0:T(8,128)(2,1)S(1)} %shard_map.117), channel_id=1, replica_groups=mesh['top'=16,'b3'=2,'b2'=2,'b1'=2,'b0'=2,'blk'=2] {'b0'}, dimensions={0}, use_global_device_ids=true | all-gather | bytes 196608 | tf_op jit(solution)/shard_map/all_gather | solution.py:388
  61.3 0.2 convolution_convert_fusion.2
  61.4 5.3 %all_gather.51.refs_1_ = bf16[256,256]{1,0:T(8,128)(2,1)S(1)} all-gather(bf16[128,256]{1,0:T(8,128)(2,1)S(1)} %convolution_convert_fusion.2), channel_id=1, replica_groups=mesh['top'=16,'b3'=2,'b2'=2,'b1'=2,'b0'=2,'blk'=2] {'b1'}, dimensions={0}, use_global_device_ids=true | all-gather | bytes 196608 | tf_op jit(solution)/shard_map/all_gather | solution.py:388
  66.7 0.2 convolution_convert_fusion.1
  66.9 3.8 %all_gather.52.refs_2_ = bf16[256,256]{1,0:T(8,128)(2,1)S(1)} all-gather(bf16[128,256]{1,0:T(8,128)(2,1)S(1)} %convolution_convert_fusion.1), channel_id=1, replica_groups=mesh['top'=16,'b3'=2,'b2'=2,'b1'=2,'b0'=2,'blk'=2] {'b2'}, dimensions={0}, use_global_device_ids=true | all-gather | bytes 196608 | tf_op jit(solution)/shard_map/all_gather | solution.py:388
  70.7 0.2 convolution_convert_fusion
  70.8 5.1 %all_gather.53.refs_3_ = bf16[256,256]{1,0:T(8,128)(2,1)S(1)} all-gather(bf16[128,256]{1,0:T(8,128)(2,1)S(1)} %convolution_convert_fusion), channel_id=1, replica_groups=mesh['top'=16,'b3'=2,'b2'=2,'b1'=2,'b0'=2,'blk'=2] {'b3'}, dimensions={0}, use_global_device_ids=true | all-gather | bytes 196608 | tf_op jit(solution)/shard_map/all_gather | solution.py:388
  75.9 7.0 %all-gather.4 = bf16[1536,256]{1,0:T(8,128)(2,1)S(1)} all-gather(bf16[768,256]{1,0:T(8,128)(2,1)S(1)} %shard_map.118), channel_id=6, replica_groups=mesh['top'=16,'b3'=2,'b2'=2,'b1'=2,'b0'=2,'blk'=2] {'blk'}, dimensions={0}, use_global_device_ids=true | all-gather | bytes 1179648 | tf_op jit(solution)/shard_map/all_gather | solution.py:333
  83.0 8.4 %shard_map.119 = (f32[512,512]{1,0:T(8,128)}, f32[512,128]{1,0:T(8,128)}, f32[1,4,256,128]{3,2,1,0:T(8,128)}) custom-call(f32[512,512]{1,0:T(8,128)S(1)} %get-tuple-element.20.direct, bf16[512,256]{1,0:T(8,128)(2,1)S(1)} %get-tuple-element.21.turned_link, bf16[2,256,512]{2,1,0:T(8,128)(2,1)S(1)} %bitcast.18, ...), custom_call_target="tpu_custom_call" | custom-call | tf_op jit(solution)/shard_map/pallas_call | solution.py:310
  (15 shorter events, 0.1 us)
Async XLA Ops:
  0.6 35.9 %copy-start = (bf16[512,512]{1,0:T(8,128)(2,1)S(1)}, bf16[512,512]{1,0:T(8,128)(2,1)}, u32[]{:S(2)}) copy-start(bf16[512,512]{1,0:T(8,128)(2,1)} %own.1) | copy-start | bytes 1572868
  0.6 27.6 %collective-permute-start.1 = (bf16[512,512]{1,0:T(8,128)(2,1)}, bf16[512,512]{1,0:T(8,128)(2,1)S(1)}, u32[]{:S(2)}, u32[]{:S(2)}) collective-permute-start(bf16[512,512]{1,0:T(8,128)(2,1)} %own.1), channel_id=1, source_target_pairs={{2,0},{4,2},{6,4},{8,6},{10,8},{12,10},{14,12},{16,14},{18,16},{20... | collective-permute-start | bytes 1572872 | tf_op jit(solution)/shard_map/ppermute | solution.py:327
  17.4 33.3 %collective-permute-start = (bf16[512,512]{1,0:T(8,128)(2,1)}, bf16[512,512]{1,0:T(8,128)(2,1)S(1)}, u32[]{:S(2)}, u32[]{:S(2)}) collective-permute-start(bf16[512,512]{1,0:T(8,128)(2,1)} %own.1), channel_id=1, source_target_pairs={{0,1},{1,0},{2,3},{3,2},{4,5},{5,4},{6,7},{7,6},{8,9},{9,8},{10,11... | collective-permute-start | bytes 1572872 | tf_op jit(solution)/shard_map/ppermute | solution.py:330
  28.3 22.4 %collective-permute-start.2 = (bf16[512,512]{1,0:T(8,128)(2,1)S(1)}, bf16[512,512]{1,0:T(8,128)(2,1)S(1)}, u32[]{:S(2)}, u32[]{:S(2)}) collective-permute-start(bf16[512,512]{1,0:T(8,128)(2,1)S(1)} %collective-permute-done.1.sketch.next_own), channel_id=1, source_target_pairs={{0,1},{1,0},{2,3},{3,2},{4,5},{5,4},{6,7},{7,6},{8,9},{9,8},{10,11... | collective-permute-start | bytes 1572872 | tf_op jit(solution)/shard_map/ppermute | solution.py:330
  31.7 16.3 %collective-permute-start.3 = (bf16[256,512]{1,0:T(8,128)(2,1)}, bf16[256,512]{1,0:T(8,128)(2,1)S(1)}, u32[]{:S(2)}, u32[]{:S(2)}) collective-permute-start(bf16[256,512]{1,0:T(8,128)(2,1)} %link.4), channel_id=1, source_target_pairs={{510,0},{0,2},{2,4},{4,6},{6,8},{8,10},{10,12},{12,14},{14,16},{16... | collective-permute-start | bytes 786440 | tf_op jit(solution)/shard_map/ppermute | solution.py:327
  34.5 2.0 %copy-start.6 = (s32[1,4,128]{2,1,0:T(4,128)S(1)}, s32[1,4,128]{2,1,0:T(4,128)}, u32[]{:S(2)}) copy-start(s32[1,4,128]{2,1,0:T(4,128)} %merge_sets.1) | copy-start | bytes 6148
  36.5 0.7 copy-start.7
  37.2 0.9 %copy-start.3 = (bf16[256,512]{1,0:T(8,128)(2,1)S(1)}, bf16[256,512]{1,0:T(8,128)(2,1)}, u32[]{:S(2)}) copy-start(bf16[256,512]{1,0:T(8,128)(2,1)} %link.5) | copy-start | bytes 786436
  38.1 2.8 %copy-start.5 = (bf16[256,512]{1,0:T(8,128)(2,1)S(1)}, bf16[256,512]{1,0:T(8,128)(2,1)}, u32[]{:S(2)}) copy-start(bf16[256,512]{1,0:T(8,128)(2,1)} %link.4) | copy-start | bytes 786436
  43.5 7.2 %copy-start.1 = (bf16[512,1024]{1,0:T(8,128)(2,1)S(1)}, bf16[512,1024]{1,0:T(8,128)(2,1)}, u32[]{:S(2)}) copy-start(bf16[512,1024]{1,0:T(8,128)(2,1)} %near.1) | copy-start | bytes 3145732
  43.5 7.2 %copy-start.2 = (bf16[512,1024]{1,0:T(8,128)(2,1)S(1)}, bf16[512,1024]{1,0:T(8,128)(2,1)}, u32[]{:S(2)}) copy-start(bf16[512,1024]{1,0:T(8,128)(2,1)} %following.1) | copy-start | bytes 3145732
  44.2 13.2 %collective-permute-start.4 = (bf16[256,256]{1,0:T(8,128)(2,1)S(1)}, bf16[256,256]{1,0:T(8,128)(2,1)S(1)}, u32[]{:S(2)}, u32[]{:S(2)}) collective-permute-start(bf16[256,256]{1,0:T(8,128)(2,1)S(1)} %shard_map.114.weights), channel_id=1, source_target_pairs={{510,0},{0,2},{2,4},{4,6},{6,8},{8,10},{10,12},{12,14},{14,16},{16... | collective-permute-start | bytes 393224 | tf_op jit(solution)/shard_map/ppermute | solution.py:327
  48.2 2.5 %copy-start.4 = (bf16[256,512]{1,0:T(8,128)(2,1)S(1)}, bf16[256,512]{1,0:T(8,128)(2,1)}, u32[]{:S(2)}) copy-start(bf16[256,512]{1,0:T(8,128)(2,1)} %link.5) | copy-start | bytes 786436

commit v2 on v1

--- a/solution.py
+++ b/solution.py
@@ -14,6 +14,18 @@
 NT = (((1,), (1,)), ((), ()))
 
 
+def crossed():
+    return lax.rem(sum(lax.axis_index(b) for b in BITS[1:]), 2)
+
+
+def own_half():
+    return lax.rem(lax.axis_index("blk") + crossed(), 2)
+
+
+def holder(half):
+    return lax.rem(half + crossed(), 2)
+
+
 def dot1(a, b, dims=NN):
     return lax.dot_general(a, b, dims, preferred_element_type=f32)
 
@@ -29,7 +41,9 @@
 
 def dot3(a, b, dims=NN):
     (ah, al), (bh, bl) = halves(a), halves(b)
-    return dot1(ah, bh, dims) + (dot1(ah, bl, dims) + dot1(al, bh, dims))
+    (over_a, over_b), _ = dims
+    left = jnp.concatenate([ah, ah, al], axis=over_a[0])
+    return dot1(left, jnp.concatenate([bh, bl, bh], axis=over_b[0]), dims)
 
 
 def iota(shape, dim):
@@ -139,7 +153,7 @@
 
 
 def load_body(base, link, sketch, kept, sent):
-    here = lax.axis_index("blk")
+    here = own_half()
     width = kept.shape[1]
     for out, half in ((kept, here), (sent, 1 - here)):
         at = pl.ds(pl.multiple_of(half * width, width), width)
@@ -148,7 +162,8 @@
 
 def split_dot(left, right):
     high, low = halves(right)
-    return dot1(left[0], high) + (dot1(left[0], low) + dot1(left[1], high))
+    wide = jnp.concatenate([left[0], left[0], left[1]], axis=1)
+    return dot1(wide, jnp.concatenate([high, low, high], axis=0))
 
 
 def solve_body(kept, got, inverse, transposed, weights):
@@ -156,10 +171,22 @@
     weights[...] = split_dot(transposed, split_dot(inverse, load)).astype(bf16)
 
 
-def carry_body(weights, previous, pick, packed):
+def carry_body(weights, previous, pick, merge_pick, packed, paths):
     rows = weights.shape[0]
     packed[:rows] = weights[...]
     packed[rows:] = dot1(pick[...], previous[...], NT).astype(bf16)
+    levels, rank = merge_pick.shape[:2]
+    paths[...] = jnp.zeros(paths.shape, bf16)
+    for j in range(levels):
+        upper = lax.axis_index(BITS[-1 - j]) == 1
+        low, high = merge_pick[j, :, :rank], merge_pick[j, :, rank:]
+        mine, theirs = jnp.where(upper, high, low), jnp.where(upper, low, high)
+        if j:
+            width = (j + 1) * rank
+            paths[j, :, :width] = dot1(mine, paths[j - 1, :, :width]).astype(bf16)
+        else:
+            paths[j, :, :rank] = mine
+        paths[j, :, (j + 1) * rank : (j + 2) * rank] = theirs
 
 
 def direct_body(
@@ -180,7 +207,7 @@
             + dot1(near[:, theirs], other[:, at])
             + dot1(following[:, mine], next_own[:, at])
             + dot1(following[:, theirs], next_other[:, at])
-            - dot1(back, carried[c, :inner])
+            - dot1(back, carried[holder(c), :inner])
         )
         direct[:, at] = part
         high, low = halves(part)
@@ -193,7 +220,7 @@
 
 
 def chosen_body(pieces, link_rows, weights, chosen):
-    here = lax.axis_index("blk")
+    here = own_half()
     count, width = chosen.shape
     at = pl.ds(pl.multiple_of(here * width, width), width)
     chosen[...] = (summed(pieces, count, at) - dot1(link_rows[...], weights[...])).astype(bf16)
@@ -250,43 +277,44 @@
 
 
 def interp_body(
-    direct, turned_link, pieces, link_rows, gathered, picks_of,
-    samples_out, leaf_interp, merge_interp, samples, gram, cross, candidates, sent,
+    direct, turned_link, pieces, link_rows, gathered, paths,
+    samples_out, leaf_out, merge_out, samples, gram, cross, ready, candidates, chosen, spun, sent,
 ):
-    levels, rank = picks_of.shape[0], gram.shape[1]
+    levels, rank = paths.shape[:2]
     width = gathered.shape[2]
-    own = slice(levels * rank, gathered.shape[1])
-    high, low = zip(*(
-        halves(
-            summed(pieces, rank, slice(c * width, (c + 1) * width))
-            - dot1(link_rows[...], gathered[c, own])
-        )
-        for c in range(2)
-    ))
-    high, low = jnp.concatenate(high, axis=1), jnp.concatenate(low, axis=1)
-    picked = []
+    theirs = levels * rank
+    every = paths[...].reshape(levels * rank, (levels + 1) * rank)
+    leaf = []
+    for c in range(2):
+        at = slice(c * width, (c + 1) * width)
+        rows = gathered[holder(c)]
+        leaf.append(halves(summed(pieces, rank, at) - dot1(link_rows[...], rows[theirs:])))
+        chosen[:, at] = (
+            dot1(every[:, :rank], leaf[c][0]) + dot1(every[:, rank:], rows[:theirs])
+        ).astype(bf16)
+    high, low = (jnp.concatenate(p, axis=1) for p in zip(*leaf))
     for j in range(levels):
-        mine = picked[-1] if picked else high
-        sibling = jnp.concatenate([gathered[c, j * rank : (j + 1) * rank] for c in range(2)], axis=1)
-        upper = lax.axis_index(BITS[-1 - j])
-        candidates[j, pl.ds(pl.multiple_of(upper * rank, rank), rank), :] = mine
-        candidates[j, pl.ds(pl.multiple_of((1 - upper) * rank, rank), rank), :] = sibling
-        picked.append(dot1(picks_of[j], candidates[j]).astype(bf16))
-    spun = [turned(rows, STEP * (j + 1)) for j, rows in enumerate(picked)]
+        rows = chosen[j * rank : (j + 1) * rank, :]
+        spun[j] = turned(rows, STEP * (j + 1))
+        gram[j + 1] = dot1(rows, spun[j], NT)
     gram[0] = dot1(high, high, NT) + (dot1(high, low, NT) + dot1(low, high, NT))
-    for j in range(levels):
-        gram[j + 1] = dot1(picked[j], spun[j], NT)
-    tall = leaf_interp.shape[0]
-    wide = merge_interp.shape[2]
+
+    def line_up():
+        for j in range(levels):
+            upper = lax.axis_index(BITS[-1 - j])
+            mine, other = (pl.ds(pl.multiple_of(u * rank, rank), rank) for u in (upper, 1 - upper))
+            candidates[j, mine, :] = chosen[(j - 1) * rank : j * rank, :] if j else high
+            for c in range(2):
+                at = slice(c * width, (c + 1) * width)
+                candidates[j, other, at] = gathered[holder(c), j * rank : (j + 1) * rank, :]
+
+    tall, wide = samples.shape[0], 2 * rank
 
     def finish():
         for c in range(2):
             at = slice(c * width, (c + 1) * width)
-            samples[:, at] = (
-                direct[:, at]
-                - dot1(turned_link[...], gathered[c, own])
-            )
-        writing.start()
+            samples[:, at] = direct[:, at] - dot1(turned_link[...], gathered[holder(c), theirs:, :])
+        writes[-1].start()
 
     def leaf_cross():
         yh, yl = halves(samples[...])
@@ -295,13 +323,20 @@
     def merge_cross(j):
         cross[tall + j * wide : tall + (j + 1) * wide] = dot1(candidates[j], spun[j], NT)
 
-    writing = pltpu.make_async_copy(samples, samples_out, sent)
-    beside = [finish, leaf_cross] + [lambda j=j: merge_cross(j) for j in range(levels)]
+    spans = [slice(0, tall)] + [slice(tall + j * wide, tall + (j + 1) * wide) for j in range(levels)]
+    targets = [leaf_out] + [merge_out.at[0, j] for j in range(levels)]
+    writes = [
+        pltpu.make_async_copy(ready.at[span], target, sent.at[i])
+        for i, (span, target) in enumerate(zip(spans, targets))
+    ]
+    writes.append(pltpu.make_async_copy(samples, samples_out, sent.at[levels + 1]))
+    beside = [finish, leaf_cross, line_up] + [lambda j=j: merge_cross(j) for j in range(levels)]
     invert_all(gram, levels + 1, rank, beside)
-    leaf_interp[...] = dot3(cross[:tall], gram[0], NT)
-    for j in range(levels):
-        merge_interp[0, j] = dot3(cross[tall + j * wide : tall + (j + 1) * wide], gram[j + 1], NT)
-    writing.wait()
+    for g, span in enumerate(spans):
+        ready[span, :] = dot3(cross[span, :], gram[g], NT)
+        writes[g].start()
+    for write in writes:
+        write.wait()
 
 
 def call(body, outs, *args, scratch=(), far=0):
@@ -325,6 +360,20 @@
     def shifted(block, distance):
         route = [((i - distance) % leaf_count, i) for i in range(leaf_count)]
         return lax.ppermute(block, leaf, route)
+
+    def on_half(block):
+        flip = [sum(i >> b & 1 for b in range(3)) % 2 for i in range(leaf_count)]
+        route = []
+        for i in range(leaf_count):
+            before = (i - 1) % leaf_count
+            route += [(2 * before + (c + flip[i] + flip[before]) % 2, 2 * i + c) for c in range(2)]
+        return lax.ppermute(block, (*leaf, "blk"), route)
+
+    def paired(block, axis):
+        if axis == BITS[0]:
+            return lax.all_gather(block, axis, axis=0, tiled=True)
+        groups = [[0, 3], [1, 2]]
+        return lax.all_gather(block, (axis, "blk"), axis=0, tiled=True, axis_index_groups=groups)
 
     def swapped(block):
         return lax.ppermute(block, "blk", [(0, 1), (1, 0)])
@@ -362,10 +411,15 @@
         )
         kept, sent = call(load_body, [((interior, half), f32)] * 2, base, link_next, next_half)
         weights = call(solve_body, [((interior, half), bf16)], kept, both(sent), inverse, transposed)
-        previous_weights = shifted(weights, 1)
+        previous_weights = on_half(weights)
         next_other = swapped(next_half)
-        packed = call(
-            carry_body, [((interior + rank, half), bf16)], weights, previous_link, leaf_pick
+        packed, paths = call(
+            carry_body,
+            [((interior + rank, half), bf16), ((levels, rank, (levels + 1) * rank), bf16)],
+            weights,
+            previous_link,
+            leaf_pick,
+            merge_pick,
         )
         direct, turned_link, pre, link_rows = call(
             direct_body,
@@ -385,7 +439,7 @@
         chosen = call(chosen_body, [((rank, half), bf16)], pieces, link_rows, previous_weights)
         pairs = []
         for level, axis in enumerate(reversed(BITS)):
-            pairs.append(lax.all_gather(chosen, axis, axis=0, tiled=True))
+            pairs.append(paired(chosen, axis))
             if level + 1 < levels:
                 chosen = dot1(merge_pick[level], pairs[-1]).astype(bf16)
         gathered = both(
@@ -399,15 +453,18 @@
             pieces,
             link_rows,
             gathered,
-            merge_pick,
+            paths,
             scratch=[
                 pltpu.VMEM((rows, cols), f32),
                 pltpu.VMEM((levels + 1, rank, rank), f32),
                 pltpu.VMEM((rows + levels * 2 * rank, rank), f32),
+                pltpu.VMEM((rows + levels * 2 * rank, rank), f32),
                 pltpu.VMEM((levels, 2 * rank, cols), bf16),
-                pltpu.SemaphoreType.DMA,
+                pltpu.VMEM((levels * rank, cols), bf16),
+                pltpu.VMEM((levels, rank, cols), bf16),
+                pltpu.SemaphoreType.DMA((levels + 2,)),
             ],
-            far=1,
+            far=3,
         )
         return samples, leaf_interp, merge_interp
 

time: 91.9 us -> 91.4 us (level)
    all_gather x5, blocking collectives: 15.8 us -> 11.4 us  [both(): return lax.all_gather(block, 'blk', axis=0)]
    all_gather x4, blocking collectives: 17.9 us -> 22.1 us  [the longest x3 15.6 us: paired(): lax.all_gather(block, (axis, 'blk'), axis=0, tiled=True, axis_index_group...]
    ppermute x0 -> x1, starting transfers between devices: none -> 2.05 us  [on_half(): return lax.ppermute(block, (*leaf, 'blk'), route)]
    ppermute x3 -> x2, starting transfers between devices: 20.6 us -> 18.6 us  [shifted(): return lax.ppermute(block, leaf, route)]
    ppermute x3 -> x2, waiting for transfers between devices: 11.6 us -> 9.8 us  [shifted(): return lax.ppermute(block, leaf, route)]
    ppermute x0 -> x1, waiting for transfers between devices: none -> 1.52 us  [on_half(): return lax.ppermute(block, (*leaf, 'blk'), route)]
  transfers between devices with their start and end apart: 5 -> 5, of which waited for: 3 -> 3; matrix products, arithmetic and copies ran while one was open for 1% -> 1% of each run, Pallas kernels for 7% -> 8%
where the time goes in v2:
time: 91.4 us; the launch traced here: 90.9 us
  blocking collectives  33.6 us (37%)
  starting transfers between devices  27 us (30%)
  Pallas kernels  15.1 us (17%)
  waiting for transfers between devices  11.3 us (12%)
  local copies, waits for them, and re-layouts  1.63 us (2%)
  between operations  0.97 us (1%)
    ppermute x2, starting transfers between devices, shifted(): return lax.ppermute(block, leaf, route)  18.6 us
    all_gather x3, blocking collectives, paired(): lax.all_gather(block, (axis, 'blk'), axis=0, tiled=True, axis_index_group...  15.6 us
    pallas_call x8, Pallas kernels, call(): pl.pallas_call(body, out_shape=shapes if len(shapes) > 1 else shapes[0],...  15.1 us
    all_gather x5, blocking collectives, both(): return lax.all_gather(block, 'blk', axis=0)  11.4 us
    ppermute x2, waiting for transfers between devices, shifted(): return lax.ppermute(block, leaf, route)  9.8 us
    all_gather x1, blocking collectives, paired(): return lax.all_gather(block, axis, axis=0, tiled=True)  6.51 us
    ppermute x2, starting transfers between devices, swapped(): return lax.ppermute(block, 'blk', [(0, 1), (1, 0)])  6.29 us
    ppermute x1, starting transfers between devices, on_half(): return lax.ppermute(block, (*leaf, 'blk'), route)  2.05 us
  transfers between devices with their start and end apart: 5, of which 3 were waited for; matrix products, arithmetic and copies ran while one was open for 1% of the time, Pallas kernels for 8%

profile of v2, /device:TPU:1, one launch (start us, length us, event | category | flops | bytes accessed | tf_op | source)
XLA Modules:
  0.0 90.9 jit_solution(9855609644579666382)
XLA Ops:
  0.6 16.7 %collective-permute-start.1 = (bf16[512,512]{1,0:T(8,128)(2,1)}, bf16[512,512]{1,0:T(8,128)(2,1)S(1)}, u32[]{:S(2)}, u32[]{:S(2)}) collective-permute-start(bf16[512,512]{1,0:T(8,128)(2,1)} %own.1), channel_id=1, source_target_pairs={{2,0},{4,2},{6,4},{8,6},{10,8},{12,10},{14,12},{16,14},{18,16},{20... | collective-permute-start | bytes 1572872 | tf_op jit(solution)/shard_map/ppermute | solution.py:362
  17.4 2.9 %collective-permute-start = (bf16[512,512]{1,0:T(8,128)(2,1)}, bf16[512,512]{1,0:T(8,128)(2,1)S(1)}, u32[]{:S(2)}, u32[]{:S(2)}) collective-permute-start(bf16[512,512]{1,0:T(8,128)(2,1)} %own.1), channel_id=1, source_target_pairs={{0,1},{1,0},{2,3},{3,2},{4,5},{5,4},{6,7},{7,6},{8,9},{9,8},{10,11... | collective-permute-start | bytes 1572872 | tf_op jit(solution)/shard_map/ppermute | solution.py:379
  20.2 8.0 %collective-permute-done.1.sketch.next_own = bf16[512,512]{1,0:T(8,128)(2,1)S(1)} collective-permute-done((bf16[512,512]{1,0:T(8,128)(2,1)}, bf16[512,512]{1,0:T(8,128)(2,1)S(1)}, u32[]{:S(2)}, u32[]{:S(2)}) %collective-permute-start.1) | collective-permute-done | bytes 524320 | tf_op jit(solution)/shard_map/ppermute | solution.py:362
  28.3 3.4 %collective-permute-start.2 = (bf16[512,512]{1,0:T(8,128)(2,1)S(1)}, bf16[512,512]{1,0:T(8,128)(2,1)S(1)}, u32[]{:S(2)}, u32[]{:S(2)}) collective-permute-start(bf16[512,512]{1,0:T(8,128)(2,1)S(1)} %collective-permute-done.1.sketch.next_own), channel_id=1, source_target_pairs={{0,1},{1,0},{2,3},{3,2},{4,5},{5,4},{6,7},{7,6},{8,9},{9,8},{10,11... | collective-permute-start | bytes 1572872 | tf_op jit(solution)/shard_map/ppermute | solution.py:379
  31.7 1.9 %collective-permute-start.3 = (bf16[256,512]{1,0:T(8,128)(2,1)}, bf16[256,512]{1,0:T(8,128)(2,1)S(1)}, u32[]{:S(2)}, u32[]{:S(2)}) collective-permute-start(bf16[256,512]{1,0:T(8,128)(2,1)} %link.4), channel_id=1, source_target_pairs={{510,0},{0,2},{2,4},{4,6},{6,8},{8,10},{10,12},{12,14},{14,16},{16... | collective-permute-start | bytes 786440 | tf_op jit(solution)/shard_map/ppermute | solution.py:362
  33.6 0.9 pad_maximum_fusion
  34.5 2.0 %all-gather = f32[512,128]{1,0:T(8,128)S(1)} all-gather(f32[256,128]{1,0:T(8,128)S(1)} %pad_maximum_fusion), channel_id=2, replica_groups=mesh['top'=16,'b3'=2,'b2'=2,'b1'=2,'b0'=2,'blk'=2] {'blk'}, dimensions={0}, use_global_device_ids=true | all-gather | bytes 393216 | tf_op jit(solution)/shard_map/all_gather | solution.py:382
  36.5 0.6 copy-done.7
  37.2 0.9 %copy-done.3 = bf16[256,512]{1,0:T(8,128)(2,1)S(1)} copy-done((bf16[256,512]{1,0:T(8,128)(2,1)S(1)}, bf16[256,512]{1,0:T(8,128)(2,1)}, u32[]{:S(2)}) %copy-start.3) | copy-done | bytes 262168
  38.1 2.8 %shard_map.112 = (bf16[2,256,256]{2,1,0:T(8,128)(2,1)S(1)}, bf16[2,256,256]{2,1,0:T(8,128)(2,1)S(1)}, f32[256,512]{1,0:T(8,128)S(1)}, bf16[128,512]{1,0:T(8,128)(2,1)S(1)}, bf16[4,128,256]{2,1,0:T(8,128)(2,1)S(1)}) custom-call(f32[2,256,128]{2,1,0:T(8,128)S(1)} %bitcast.22, bf16[256,512]{1,0:T(8,128)(2,1)S(1)} %copy-done.3, bf16[512,512]{1,0:T(8,128)(2,1)S(1)} %copy-done, ...), custom_call_target="tpu_custom_call" | custom-call | tf_op jit(solution)/shard_map/pallas_call | solution.py:345
  41.0 0.3 shard_map.113
  41.3 2.2 %all-gather.1 = f32[512,256]{1,0:T(8,128)S(1)} all-gather(f32[256,256]{1,0:T(8,128)S(1)} %get-tuple-element.18), channel_id=3, replica_groups=mesh['top'=16,'b3'=2,'b2'=2,'b1'=2,'b0'=2,'blk'=2] {'blk'}, dimensions={0}, use_global_device_ids=true | all-gather | bytes 786432 | tf_op jit(solution)/shard_map/all_gather | solution.py:382
  43.5 0.7 shard_map.114.weights
  44.2 0.0 copy-start.1
  44.2 2.1 %collective-permute-start.4 = (bf16[256,256]{1,0:T(8,128)(2,1)S(1)}, bf16[256,256]{1,0:T(8,128)(2,1)S(1)}, u32[]{:S(2)}, u32[]{:S(2)}) collective-permute-start(bf16[256,256]{1,0:T(8,128)(2,1)S(1)} %shard_map.114.weights), channel_id=1, source_target_pairs={{511,0},{510,1},{1,2},{0,3},{2,4},{3,5},{5,6},{4,7},{7,8},{6,9},{9... | collective-permute-start | bytes 393224 | tf_op jit(solution)/shard_map/ppermute | solution.py:370
  46.2 1.8 %collective-permute-done.3.previous = bf16[256,512]{1,0:T(8,128)(2,1)S(1)} collective-permute-done((bf16[256,512]{1,0:T(8,128)(2,1)}, bf16[256,512]{1,0:T(8,128)(2,1)S(1)}, u32[]{:S(2)}, u32[]{:S(2)}) %collective-permute-start.3) | collective-permute-done | bytes 262176 | tf_op jit(solution)/shard_map/ppermute | solution.py:362
  48.0 0.5 shard_map.115
  48.6 0.0 copy-start.4
  48.6 2.4 %all-gather.2 = bf16[768,256]{1,0:T(8,128)(2,1)S(1)} all-gather(bf16[384,256]{1,0:T(8,128)(2,1)S(1)} %get-tuple-element.23), channel_id=4, replica_groups=mesh['top'=16,'b3'=2,'b2'=2,'b1'=2,'b0'=2,'blk'=2] {'blk'}, dimensions={0}, use_global_device_ids=true | all-gather | bytes 589824 | tf_op jit(solution)/shard_map/all_gather | solution.py:382
  51.0 2.8 %shard_map.116 = (f32[512,512]{1,0:T(8,128)S(1)}, bf16[512,256]{1,0:T(8,128)(2,1)S(1)}, bf16[256,512]{1,0:T(8,128)(2,1)S(1)}, bf16[128,256]{1,0:T(8,128)(2,1)S(1)}) custom-call(bf16[512,1024]{1,0:T(8,128)(2,1)S(1)} %copy-done.1, bf16[512,1024]{1,0:T(8,128)(2,1)S(1)} %copy-done.2, bf16[512,512]{1,0:T(8,128)(2,1)S(1)} %copy-done, ...), custom_call_target="tpu_custom_call" | custom-call | tf_op jit(solution)/shard_map/pallas_call | solution.py:345
  53.8 2.2 %all-gather.3 = bf16[512,512]{1,0:T(8,128)(2,1)S(1)} all-gather(bf16[256,512]{1,0:T(8,128)(2,1)S(1)} %get-tuple-element.26), channel_id=5, replica_groups=mesh['top'=16,'b3'=2,'b2'=2,'b1'=2,'b0'=2,'blk'=2] {'blk'}, dimensions={0}, use_global_device_ids=true | all-gather | bytes 786432 | tf_op jit(solution)/shard_map/all_gather | solution.py:382
  56.0 1.5 %collective-permute-done.4.weights = bf16[256,256]{1,0:T(8,128)(2,1)S(1)} collective-permute-done((bf16[256,256]{1,0:T(8,128)(2,1)S(1)}, bf16[256,256]{1,0:T(8,128)(2,1)S(1)}, u32[]{:S(2)}, u32[]{:S(2)}) %collective-permute-start.4) | collective-permute-done | bytes 131104 | tf_op jit(solution)/shard_map/ppermute | solution.py:370
  57.5 0.2 shard_map.117
  57.7 4.7 %all_gather.50.refs_0_ = bf16[256,256]{1,0:T(8,128)(2,1)S(1)} all-gather(bf16[128,256]{1,0:T(8,128)(2,1)S(1)} %shard_map.117), channel_id=1, replica_groups={{0,3},{1,2},{4,7},{5,6},{8,11},{9,10},{12,15},{13,14},{16,19},{17,18},{..., dimensions={0}, use_global_device_ids=true | all-gather | bytes 196608 | tf_op jit(solution)/shard_map/all_gather | solution.py:376
  62.4 0.2 convolution_convert_fusion.2
  62.6 6.2 %all_gather.51.refs_1_ = bf16[256,256]{1,0:T(8,128)(2,1)S(1)} all-gather(bf16[128,256]{1,0:T(8,128)(2,1)S(1)} %convolution_convert_fusion.2), channel_id=1, replica_groups={{0,5},{1,4},{2,7},{3,6},{8,13},{9,12},{10,15},{11,14},{16,21},{17,20},{..., dimensions={0}, use_global_device_ids=true | all-gather | bytes 196608 | tf_op jit(solution)/shard_map/all_gather | solution.py:376
  68.8 0.2 convolution_convert_fusion.1
  69.0 4.7 %all_gather.52.refs_2_ = bf16[256,256]{1,0:T(8,128)(2,1)S(1)} all-gather(bf16[128,256]{1,0:T(8,128)(2,1)S(1)} %convolution_convert_fusion.1), channel_id=1, replica_groups={{0,9},{1,8},{2,11},{3,10},{4,13},{5,12},{6,15},{7,14},{16,25},{17,24},{..., dimensions={0}, use_global_device_ids=true | all-gather | bytes 196608 | tf_op jit(solution)/shard_map/all_gather | solution.py:376
  73.6 0.2 convolution_convert_fusion
  73.8 6.5 %all_gather.53.refs_3_ = bf16[256,256]{1,0:T(8,128)(2,1)S(1)} all-gather(bf16[128,256]{1,0:T(8,128)(2,1)S(1)} %convolution_convert_fusion), channel_id=1, replica_groups=mesh['top'=16,'b3'=2,'b2'=2,'b1'=2,'b0'=2,'blk'=2] {'b3'}, dimensions={0}, use_global_device_ids=true | all-gather | bytes 196608 | tf_op jit(solution)/shard_map/all_gather | solution.py:374
  80.3 2.6 %all-gather.4 = bf16[1536,256]{1,0:T(8,128)(2,1)S(1)} all-gather(bf16[768,256]{1,0:T(8,128)(2,1)S(1)} %shard_map.118), channel_id=6, replica_groups=mesh['top'=16,'b3'=2,'b2'=2,'b1'=2,'b0'=2,'blk'=2] {'blk'}, dimensions={0}, use_global_device_ids=true | all-gather | bytes 1179648 | tf_op jit(solution)/shard_map/all_gather | solution.py:382
  83.0 7.8 %shard_map.119 = (f32[512,512]{1,0:T(8,128)}, f32[512,128]{1,0:T(8,128)}, f32[1,4,256,128]{3,2,1,0:T(8,128)}) custom-call(f32[512,512]{1,0:T(8,128)S(1)} %get-tuple-element.24.direct, bf16[512,256]{1,0:T(8,128)(2,1)S(1)} %get-tuple-element.25.turned_link, bf16[2,256,512]{2,1,0:T(8,128)(2,1)S(1)} %bitcast.18, ...), custom_call_target="tpu_custom_call" | custom-call | tf_op jit(solution)/shard_map/pallas_call | solution.py:345
  (15 shorter events, 0.1 us)
Async XLA Ops:
  0.6 35.9 %copy-start = (bf16[512,512]{1,0:T(8,128)(2,1)S(1)}, bf16[512,512]{1,0:T(8,128)(2,1)}, u32[]{:S(2)}) copy-start(bf16[512,512]{1,0:T(8,128)(2,1)} %own.1) | copy-start | bytes 1572868
  0.6 27.6 %collective-permute-start.1 = (bf16[512,512]{1,0:T(8,128)(2,1)}, bf16[512,512]{1,0:T(8,128)(2,1)S(1)}, u32[]{:S(2)}, u32[]{:S(2)}) collective-permute-start(bf16[512,512]{1,0:T(8,128)(2,1)} %own.1), channel_id=1, source_target_pairs={{2,0},{4,2},{6,4},{8,6},{10,8},{12,10},{14,12},{16,14},{18,16},{20... | collective-permute-start | bytes 1572872 | tf_op jit(solution)/shard_map/ppermute | solution.py:362
  17.4 33.6 %collective-permute-start = (bf16[512,512]{1,0:T(8,128)(2,1)}, bf16[512,512]{1,0:T(8,128)(2,1)S(1)}, u32[]{:S(2)}, u32[]{:S(2)}) collective-permute-start(bf16[512,512]{1,0:T(8,128)(2,1)} %own.1), channel_id=1, source_target_pairs={{0,1},{1,0},{2,3},{3,2},{4,5},{5,4},{6,7},{7,6},{8,9},{9,8},{10,11... | collective-permute-start | bytes 1572872 | tf_op jit(solution)/shard_map/ppermute | solution.py:379
  28.3 22.7 %collective-permute-start.2 = (bf16[512,512]{1,0:T(8,128)(2,1)S(1)}, bf16[512,512]{1,0:T(8,128)(2,1)S(1)}, u32[]{:S(2)}, u32[]{:S(2)}) collective-permute-start(bf16[512,512]{1,0:T(8,128)(2,1)S(1)} %collective-permute-done.1.sketch.next_own), channel_id=1, source_target_pairs={{0,1},{1,0},{2,3},{3,2},{4,5},{5,4},{6,7},{7,6},{8,9},{9,8},{10,11... | collective-permute-start | bytes 1572872 | tf_op jit(solution)/shard_map/ppermute | solution.py:379
  31.7 16.3 %collective-permute-start.3 = (bf16[256,512]{1,0:T(8,128)(2,1)}, bf16[256,512]{1,0:T(8,128)(2,1)S(1)}, u32[]{:S(2)}, u32[]{:S(2)}) collective-permute-start(bf16[256,512]{1,0:T(8,128)(2,1)} %link.4), channel_id=1, source_target_pairs={{510,0},{0,2},{2,4},{4,6},{6,8},{8,10},{10,12},{12,14},{14,16},{16... | collective-permute-start | bytes 786440 | tf_op jit(solution)/shard_map/ppermute | solution.py:362
  34.5 2.0 %copy-start.6 = (s32[1,4,128]{2,1,0:T(4,128)S(1)}, s32[1,4,128]{2,1,0:T(4,128)}, u32[]{:S(2)}) copy-start(s32[1,4,128]{2,1,0:T(4,128)} %merge_sets.1) | copy-start | bytes 6148
  36.5 0.7 copy-start.7
  37.2 0.9 %copy-start.3 = (bf16[256,512]{1,0:T(8,128)(2,1)S(1)}, bf16[256,512]{1,0:T(8,128)(2,1)}, u32[]{:S(2)}) copy-start(bf16[256,512]{1,0:T(8,128)(2,1)} %link.5) | copy-start | bytes 786436
  38.1 2.8 %copy-start.5 = (bf16[256,512]{1,0:T(8,128)(2,1)S(1)}, bf16[256,512]{1,0:T(8,128)(2,1)}, u32[]{:S(2)}) copy-start(bf16[256,512]{1,0:T(8,128)(2,1)} %link.4) | copy-start | bytes 786436
  43.5 7.5 %copy-start.2 = (bf16[512,1024]{1,0:T(8,128)(2,1)S(1)}, bf16[512,1024]{1,0:T(8,128)(2,1)}, u32[]{:S(2)}) copy-start(bf16[512,1024]{1,0:T(8,128)(2,1)} %following.1) | copy-start | bytes 3145732
  44.2 6.8 %copy-start.1 = (bf16[512,1024]{1,0:T(8,128)(2,1)S(1)}, bf16[512,1024]{1,0:T(8,128)(2,1)}, u32[]{:S(2)}) copy-start(bf16[512,1024]{1,0:T(8,128)(2,1)} %near.1) | copy-start | bytes 3145732
  44.2 13.3 %collective-permute-start.4 = (bf16[256,256]{1,0:T(8,128)(2,1)S(1)}, bf16[256,256]{1,0:T(8,128)(2,1)S(1)}, u32[]{:S(2)}, u32[]{:S(2)}) collective-permute-start(bf16[256,256]{1,0:T(8,128)(2,1)S(1)} %shard_map.114.weights), channel_id=1, source_target_pairs={{511,0},{510,1},{1,2},{0,3},{2,4},{3,5},{5,6},{4,7},{7,8},{6,9},{9... | collective-permute-start | bytes 393224 | tf_op jit(solution)/shard_map/ppermute | solution.py:370
  48.6 2.5 %copy-start.4 = (bf16[256,512]{1,0:T(8,128)(2,1)S(1)}, bf16[256,512]{1,0:T(8,128)(2,1)}, u32[]{:S(2)}) copy-start(bf16[256,512]{1,0:T(8,128)(2,1)} %link.5) | copy-start | bytes 786436

commit v3 on v2

--- a/solution.py
+++ b/solution.py
@@ -226,13 +226,14 @@
     chosen[...] = (summed(pieces, count, at) - dot1(link_rows[...], weights[...])).astype(bf16)
 
 
-def pack_body(weights, *refs):
+def pack_body(weights, leaf, *refs):
     pairs, packed = refs[:-1], refs[-1]
     rank = pairs[0].shape[0] // 2
     for j, pair in enumerate(pairs):
         other = 1 - lax.axis_index(BITS[-1 - j])
         packed[j * rank : (j + 1) * rank] = pair[pl.ds(pl.multiple_of(other * rank, rank), rank), :]
-    packed[len(pairs) * rank :] = weights[...]
+    packed[len(pairs) * rank : (len(pairs) + 1) * rank] = leaf[...]
+    packed[(len(pairs) + 1) * rank :] = weights[...]
 
 
 def turned(rows, by):
@@ -253,8 +254,6 @@
         for g, q in enumerate(places):
             packed = jnp.where(group == q, panels[g], packed)
         pivots = block_rows(group_inverse(packed))
-        if k < len(beside):
-            beside[k]()
         stacked = [jnp.zeros((STEP, size), f32)] * groups
         for g, q in enumerate(places):
             stacked[q] = panels[g]
@@ -269,6 +268,8 @@
                 jnp.where(group == q, 0.0, a) - change[g * STEP : (g + 1) * STEP]
                 for g, (q, a) in enumerate(zip(places, ahead))
             ]
+        if k < len(beside):
+            beside[k]()
         left = [jnp.where(wide_group == q, gram[g], 0.0) for g, q in enumerate(places)]
         change = dot3(jnp.concatenate(left, axis=0), scaled)
         for g, q in enumerate(places):
@@ -282,21 +283,27 @@
 ):
     levels, rank = paths.shape[:2]
     width = gathered.shape[2]
-    theirs = levels * rank
+    siblings, theirs = levels * rank, (levels + 1) * rank
     every = paths[...].reshape(levels * rank, (levels + 1) * rank)
-    leaf = []
-    for c in range(2):
-        at = slice(c * width, (c + 1) * width)
-        rows = gathered[holder(c)]
-        leaf.append(halves(summed(pieces, rank, at) - dot1(link_rows[...], rows[theirs:])))
+    halves_at = [slice(c * width, (c + 1) * width) for c in range(2)]
+    for c, at in enumerate(halves_at):
         chosen[:, at] = (
-            dot1(every[:, :rank], leaf[c][0]) + dot1(every[:, rank:], rows[:theirs])
+            dot1(every[:, :rank], gathered[holder(c), siblings:theirs, :])
+            + dot1(every[:, rank:], gathered[holder(c), :siblings, :])
         ).astype(bf16)
-    high, low = (jnp.concatenate(p, axis=1) for p in zip(*leaf))
     for j in range(levels):
         rows = chosen[j * rank : (j + 1) * rank, :]
         spun[j] = turned(rows, STEP * (j + 1))
         gram[j + 1] = dot1(rows, spun[j], NT)
+    high = jnp.concatenate([gathered[holder(c), siblings:theirs, :] for c in range(2)], axis=1)
+    low = jnp.concatenate(
+        [
+            summed(pieces, rank, at) - dot1(link_rows[...], gathered[holder(c), theirs:, :])
+            for c, at in enumerate(halves_at)
+        ],
+        axis=1,
+    )
+    low = (low - high.astype(f32)).astype(bf16)
     gram[0] = dot1(high, high, NT) + (dot1(high, low, NT) + dot1(low, high, NT))
 
     def line_up():
@@ -437,13 +444,20 @@
         )
         pieces = both(pre)
         chosen = call(chosen_body, [((rank, half), bf16)], pieces, link_rows, previous_weights)
+        leaf_rows = chosen
         pairs = []
         for level, axis in enumerate(reversed(BITS)):
             pairs.append(paired(chosen, axis))
             if level + 1 < levels:
                 chosen = dot1(merge_pick[level], pairs[-1]).astype(bf16)
         gathered = both(
-            call(pack_body, [((levels * rank + interior, half), bf16)], previous_weights, *pairs)
+            call(
+                pack_body,
+                [(((levels + 1) * rank + interior, half), bf16)],
+                previous_weights,
+                leaf_rows,
+                *pairs,
+            )
         )
         samples, leaf_interp, merge_interp = call(
             interp_body,

time: 91.4 us -> 91.1 us (level)
  no operation moved by 1% of the time
where the time goes in v3:
time: 91.1 us; the launch traced here: 90.6 us
  blocking collectives  33.5 us (37%)
  starting transfers between devices  27 us (30%)
  Pallas kernels  15.1 us (17%)
  waiting for transfers between devices  11.3 us (12%)
  local copies, waits for them, and re-layouts  1.63 us (2%)
    ppermute x2, starting transfers between devices, shifted(): return lax.ppermute(block, leaf, route)  18.6 us
    all_gather x3, blocking collectives, paired(): lax.all_gather(block, (axis, 'blk'), axis=0, tiled=True, axis_index_group...  15.6 us
    pallas_call x8, Pallas kernels, call(): pl.pallas_call(body, out_shape=shapes if len(shapes) > 1 else shapes[0],...  15.1 us
    all_gather x5, blocking collectives, both(): return lax.all_gather(block, 'blk', axis=0)  11.4 us
    ppermute x2, waiting for transfers between devices, shifted(): return lax.ppermute(block, leaf, route)  9.8 us
    all_gather x1, blocking collectives, paired(): return lax.all_gather(block, axis, axis=0, tiled=True)  6.52 us
    ppermute x2, starting transfers between devices, swapped(): return lax.ppermute(block, 'blk', [(0, 1), (1, 0)])  6.29 us
    ppermute x1, starting transfers between devices, on_half(): return lax.ppermute(block, (*leaf, 'blk'), route)  2.05 us
  transfers between devices with their start and end apart: 5, of which 3 were waited for; matrix products, arithmetic and copies ran while one was open for 1% of the time, Pallas kernels for 8%

profile of v3, /device:TPU:1, one launch (start us, length us, event | category | flops | bytes accessed | tf_op | source)
XLA Modules:
  0.0 90.6 jit_solution(7221776622266374482)
XLA Ops:
  0.6 16.7 %collective-permute-start.1 = (bf16[512,512]{1,0:T(8,128)(2,1)}, bf16[512,512]{1,0:T(8,128)(2,1)S(1)}, u32[]{:S(2)}, u32[]{:S(2)}) collective-permute-start(bf16[512,512]{1,0:T(8,128)(2,1)} %own.1), channel_id=1, source_target_pairs={{2,0},{4,2},{6,4},{8,6},{10,8},{12,10},{14,12},{16,14},{18,16},{20... | collective-permute-start | bytes 1572872 | tf_op jit(solution)/shard_map/ppermute | solution.py:369
  17.4 2.9 %collective-permute-start = (bf16[512,512]{1,0:T(8,128)(2,1)}, bf16[512,512]{1,0:T(8,128)(2,1)S(1)}, u32[]{:S(2)}, u32[]{:S(2)}) collective-permute-start(bf16[512,512]{1,0:T(8,128)(2,1)} %own.1), channel_id=1, source_target_pairs={{0,1},{1,0},{2,3},{3,2},{4,5},{5,4},{6,7},{7,6},{8,9},{9,8},{10,11... | collective-permute-start | bytes 1572872 | tf_op jit(solution)/shard_map/ppermute | solution.py:386
  20.2 8.0 %collective-permute-done.1.sketch.next_own = bf16[512,512]{1,0:T(8,128)(2,1)S(1)} collective-permute-done((bf16[512,512]{1,0:T(8,128)(2,1)}, bf16[512,512]{1,0:T(8,128)(2,1)S(1)}, u32[]{:S(2)}, u32[]{:S(2)}) %collective-permute-start.1) | collective-permute-done | bytes 524320 | tf_op jit(solution)/shard_map/ppermute | solution.py:369
  28.3 3.4 %collective-permute-start.2 = (bf16[512,512]{1,0:T(8,128)(2,1)S(1)}, bf16[512,512]{1,0:T(8,128)(2,1)S(1)}, u32[]{:S(2)}, u32[]{:S(2)}) collective-permute-start(bf16[512,512]{1,0:T(8,128)(2,1)S(1)} %collective-permute-done.1.sketch.next_own), channel_id=1, source_target_pairs={{0,1},{1,0},{2,3},{3,2},{4,5},{5,4},{6,7},{7,6},{8,9},{9,8},{10,11... | collective-permute-start | bytes 1572872 | tf_op jit(solution)/shard_map/ppermute | solution.py:386
  31.7 1.9 %collective-permute-start.3 = (bf16[256,512]{1,0:T(8,128)(2,1)}, bf16[256,512]{1,0:T(8,128)(2,1)S(1)}, u32[]{:S(2)}, u32[]{:S(2)}) collective-permute-start(bf16[256,512]{1,0:T(8,128)(2,1)} %link.4), channel_id=1, source_target_pairs={{510,0},{0,2},{2,4},{4,6},{6,8},{8,10},{10,12},{12,14},{14,16},{16... | collective-permute-start | bytes 786440 | tf_op jit(solution)/shard_map/ppermute | solution.py:369
  33.6 0.9 pad_maximum_fusion
  34.5 0.0 copy-start.6
  34.5 2.0 %all-gather = f32[512,128]{1,0:T(8,128)S(1)} all-gather(f32[256,128]{1,0:T(8,128)S(1)} %pad_maximum_fusion), channel_id=2, replica_groups=mesh['top'=16,'b3'=2,'b2'=2,'b1'=2,'b0'=2,'blk'=2] {'blk'}, dimensions={0}, use_global_device_ids=true | all-gather | bytes 393216 | tf_op jit(solution)/shard_map/all_gather | solution.py:389
  36.5 0.6 copy-done.7
  37.2 0.9 %copy-done.3 = bf16[256,512]{1,0:T(8,128)(2,1)S(1)} copy-done((bf16[256,512]{1,0:T(8,128)(2,1)S(1)}, bf16[256,512]{1,0:T(8,128)(2,1)}, u32[]{:S(2)}) %copy-start.3) | copy-done | bytes 262168
  38.1 2.8 %shard_map.112 = (bf16[2,256,256]{2,1,0:T(8,128)(2,1)S(1)}, bf16[2,256,256]{2,1,0:T(8,128)(2,1)S(1)}, f32[256,512]{1,0:T(8,128)S(1)}, bf16[128,512]{1,0:T(8,128)(2,1)S(1)}, bf16[4,128,256]{2,1,0:T(8,128)(2,1)S(1)}) custom-call(f32[2,256,128]{2,1,0:T(8,128)S(1)} %bitcast.22, bf16[256,512]{1,0:T(8,128)(2,1)S(1)} %copy-done.3, bf16[512,512]{1,0:T(8,128)(2,1)S(1)} %copy-done, ...), custom_call_target="tpu_custom_call" | custom-call | tf_op jit(solution)/shard_map/pallas_call | solution.py:352
  41.0 0.3 shard_map.113
  41.3 2.2 %all-gather.1 = f32[512,256]{1,0:T(8,128)S(1)} all-gather(f32[256,256]{1,0:T(8,128)S(1)} %get-tuple-element.18), channel_id=3, replica_groups=mesh['top'=16,'b3'=2,'b2'=2,'b1'=2,'b0'=2,'blk'=2] {'blk'}, dimensions={0}, use_global_device_ids=true | all-gather | bytes 786432 | tf_op jit(solution)/shard_map/all_gather | solution.py:389
  43.5 0.7 shard_map.114.weights
  44.2 0.0 copy-start.1
  44.2 2.1 %collective-permute-start.4 = (bf16[256,256]{1,0:T(8,128)(2,1)S(1)}, bf16[256,256]{1,0:T(8,128)(2,1)S(1)}, u32[]{:S(2)}, u32[]{:S(2)}) collective-permute-start(bf16[256,256]{1,0:T(8,128)(2,1)S(1)} %shard_map.114.weights), channel_id=1, source_target_pairs={{511,0},{510,1},{1,2},{0,3},{2,4},{3,5},{5,6},{4,7},{7,8},{6,9},{9... | collective-permute-start | bytes 393224 | tf_op jit(solution)/shard_map/ppermute | solution.py:377
  46.2 1.8 %collective-permute-done.3.previous = bf16[256,512]{1,0:T(8,128)(2,1)S(1)} collective-permute-done((bf16[256,512]{1,0:T(8,128)(2,1)}, bf16[256,512]{1,0:T(8,128)(2,1)S(1)}, u32[]{:S(2)}, u32[]{:S(2)}) %collective-permute-start.3) | collective-permute-done | bytes 262176 | tf_op jit(solution)/shard_map/ppermute | solution.py:369
  48.0 0.5 shard_map.115
  48.6 2.4 %all-gather.2 = bf16[768,256]{1,0:T(8,128)(2,1)S(1)} all-gather(bf16[384,256]{1,0:T(8,128)(2,1)S(1)} %get-tuple-element.23), channel_id=4, replica_groups=mesh['top'=16,'b3'=2,'b2'=2,'b1'=2,'b0'=2,'blk'=2] {'blk'}, dimensions={0}, use_global_device_ids=true | all-gather | bytes 589824 | tf_op jit(solution)/shard_map/all_gather | solution.py:389
  51.0 2.8 %shard_map.116 = (f32[512,512]{1,0:T(8,128)S(1)}, bf16[512,256]{1,0:T(8,128)(2,1)S(1)}, bf16[256,512]{1,0:T(8,128)(2,1)S(1)}, bf16[128,256]{1,0:T(8,128)(2,1)S(1)}) custom-call(bf16[512,1024]{1,0:T(8,128)(2,1)S(1)} %copy-done.1, bf16[512,1024]{1,0:T(8,128)(2,1)S(1)} %copy-done.2, bf16[512,512]{1,0:T(8,128)(2,1)S(1)} %copy-done, ...), custom_call_target="tpu_custom_call" | custom-call | tf_op jit(solution)/shard_map/pallas_call | solution.py:352
  53.8 2.2 %all-gather.3 = bf16[512,512]{1,0:T(8,128)(2,1)S(1)} all-gather(bf16[256,512]{1,0:T(8,128)(2,1)S(1)} %get-tuple-element.26), channel_id=5, replica_groups=mesh['top'=16,'b3'=2,'b2'=2,'b1'=2,'b0'=2,'blk'=2] {'blk'}, dimensions={0}, use_global_device_ids=true | all-gather | bytes 786432 | tf_op jit(solution)/shard_map/all_gather | solution.py:389
  56.0 1.5 %collective-permute-done.4.weights = bf16[256,256]{1,0:T(8,128)(2,1)S(1)} collective-permute-done((bf16[256,256]{1,0:T(8,128)(2,1)S(1)}, bf16[256,256]{1,0:T(8,128)(2,1)S(1)}, u32[]{:S(2)}, u32[]{:S(2)}) %collective-permute-start.4) | collective-permute-done | bytes 131104 | tf_op jit(solution)/shard_map/ppermute | solution.py:377
  57.5 0.2 shard_map.117.leaf
  57.7 4.7 %all_gather.50.refs_0_ = bf16[256,256]{1,0:T(8,128)(2,1)S(1)} all-gather(bf16[128,256]{1,0:T(8,128)(2,1)S(1)} %shard_map.117.leaf), channel_id=1, replica_groups={{0,3},{1,2},{4,7},{5,6},{8,11},{9,10},{12,15},{13,14},{16,19},{17,18},{..., dimensions={0}, use_global_device_ids=true | all-gather | bytes 196608 | tf_op jit(solution)/shard_map/all_gather | solution.py:383
  62.4 0.2 convolution_convert_fusion.2
  62.6 6.2 %all_gather.51.refs_1_ = bf16[256,256]{1,0:T(8,128)(2,1)S(1)} all-gather(bf16[128,256]{1,0:T(8,128)(2,1)S(1)} %convolution_convert_fusion.2), channel_id=1, replica_groups={{0,5},{1,4},{2,7},{3,6},{8,13},{9,12},{10,15},{11,14},{16,21},{17,20},{..., dimensions={0}, use_global_device_ids=true | all-gather | bytes 196608 | tf_op jit(solution)/shard_map/all_gather | solution.py:383
  68.8 0.2 convolution_convert_fusion.1
  68.9 4.7 %all_gather.52.refs_2_ = bf16[256,256]{1,0:T(8,128)(2,1)S(1)} all-gather(bf16[128,256]{1,0:T(8,128)(2,1)S(1)} %convolution_convert_fusion.1), channel_id=1, replica_groups={{0,9},{1,8},{2,11},{3,10},{4,13},{5,12},{6,15},{7,14},{16,25},{17,24},{..., dimensions={0}, use_global_device_ids=true | all-gather | bytes 196608 | tf_op jit(solution)/shard_map/all_gather | solution.py:383
  73.6 0.2 convolution_convert_fusion
  73.8 6.5 %all_gather.53.refs_3_ = bf16[256,256]{1,0:T(8,128)(2,1)S(1)} all-gather(bf16[128,256]{1,0:T(8,128)(2,1)S(1)} %convolution_convert_fusion), channel_id=1, replica_groups=mesh['top'=16,'b3'=2,'b2'=2,'b1'=2,'b0'=2,'blk'=2] {'b3'}, dimensions={0}, use_global_device_ids=true | all-gather | bytes 196608 | tf_op jit(solution)/shard_map/all_gather | solution.py:381
  80.3 2.6 %all-gather.4 = bf16[1792,256]{1,0:T(8,128)(2,1)S(1)} all-gather(bf16[896,256]{1,0:T(8,128)(2,1)S(1)} %shard_map.118), channel_id=6, replica_groups=mesh['top'=16,'b3'=2,'b2'=2,'b1'=2,'b0'=2,'blk'=2] {'blk'}, dimensions={0}, use_global_device_ids=true | all-gather | bytes 1376256 | tf_op jit(solution)/shard_map/all_gather | solution.py:389
  82.9 7.7 %shard_map.119 = (f32[512,512]{1,0:T(8,128)}, f32[512,128]{1,0:T(8,128)}, f32[1,4,256,128]{3,2,1,0:T(8,128)}) custom-call(f32[512,512]{1,0:T(8,128)S(1)} %get-tuple-element.24.direct, bf16[512,256]{1,0:T(8,128)(2,1)S(1)} %get-tuple-element.25.turned_link, bf16[2,256,512]{2,1,0:T(8,128)(2,1)S(1)} %bitcast.18, ...), custom_call_target="tpu_custom_call" | custom-call | tf_op jit(solution)/shard_map/pallas_call | solution.py:352
  (15 shorter events, 0.1 us)
Async XLA Ops:
  0.6 35.9 %copy-start = (bf16[512,512]{1,0:T(8,128)(2,1)S(1)}, bf16[512,512]{1,0:T(8,128)(2,1)}, u32[]{:S(2)}) copy-start(bf16[512,512]{1,0:T(8,128)(2,1)} %own.1) | copy-start | bytes 1572868
  0.6 27.6 %collective-permute-start.1 = (bf16[512,512]{1,0:T(8,128)(2,1)}, bf16[512,512]{1,0:T(8,128)(2,1)S(1)}, u32[]{:S(2)}, u32[]{:S(2)}) collective-permute-start(bf16[512,512]{1,0:T(8,128)(2,1)} %own.1), channel_id=1, source_target_pairs={{2,0},{4,2},{6,4},{8,6},{10,8},{12,10},{14,12},{16,14},{18,16},{20... | collective-permute-start | bytes 1572872 | tf_op jit(solution)/shard_map/ppermute | solution.py:369
  17.4 33.6 %collective-permute-start = (bf16[512,512]{1,0:T(8,128)(2,1)}, bf16[512,512]{1,0:T(8,128)(2,1)S(1)}, u32[]{:S(2)}, u32[]{:S(2)}) collective-permute-start(bf16[512,512]{1,0:T(8,128)(2,1)} %own.1), channel_id=1, source_target_pairs={{0,1},{1,0},{2,3},{3,2},{4,5},{5,4},{6,7},{7,6},{8,9},{9,8},{10,11... | collective-permute-start | bytes 1572872 | tf_op jit(solution)/shard_map/ppermute | solution.py:386
  28.3 22.7 %collective-permute-start.2 = (bf16[512,512]{1,0:T(8,128)(2,1)S(1)}, bf16[512,512]{1,0:T(8,128)(2,1)S(1)}, u32[]{:S(2)}, u32[]{:S(2)}) collective-permute-start(bf16[512,512]{1,0:T(8,128)(2,1)S(1)} %collective-permute-done.1.sketch.next_own), channel_id=1, source_target_pairs={{0,1},{1,0},{2,3},{3,2},{4,5},{5,4},{6,7},{7,6},{8,9},{9,8},{10,11... | collective-permute-start | bytes 1572872 | tf_op jit(solution)/shard_map/ppermute | solution.py:386
  31.7 16.3 %collective-permute-start.3 = (bf16[256,512]{1,0:T(8,128)(2,1)}, bf16[256,512]{1,0:T(8,128)(2,1)S(1)}, u32[]{:S(2)}, u32[]{:S(2)}) collective-permute-start(bf16[256,512]{1,0:T(8,128)(2,1)} %link.4), channel_id=1, source_target_pairs={{510,0},{0,2},{2,4},{4,6},{6,8},{8,10},{10,12},{12,14},{14,16},{16... | collective-permute-start | bytes 786440 | tf_op jit(solution)/shard_map/ppermute | solution.py:369
  34.5 2.0 %copy-start.6 = (s32[1,4,128]{2,1,0:T(4,128)S(1)}, s32[1,4,128]{2,1,0:T(4,128)}, u32[]{:S(2)}) copy-start(s32[1,4,128]{2,1,0:T(4,128)} %merge_sets.1) | copy-start | bytes 6148
  36.5 0.7 copy-start.7
  37.2 0.9 %copy-start.3 = (bf16[256,512]{1,0:T(8,128)(2,1)S(1)}, bf16[256,512]{1,0:T(8,128)(2,1)}, u32[]{:S(2)}) copy-start(bf16[256,512]{1,0:T(8,128)(2,1)} %link.5) | copy-start | bytes 786436
  38.1 2.8 %copy-start.5 = (bf16[256,512]{1,0:T(8,128)(2,1)S(1)}, bf16[256,512]{1,0:T(8,128)(2,1)}, u32[]{:S(2)}) copy-start(bf16[256,512]{1,0:T(8,128)(2,1)} %link.4) | copy-start | bytes 786436
  43.5 7.5 %copy-start.2 = (bf16[512,1024]{1,0:T(8,128)(2,1)S(1)}, bf16[512,1024]{1,0:T(8,128)(2,1)}, u32[]{:S(2)}) copy-start(bf16[512,1024]{1,0:T(8,128)(2,1)} %following.1) | copy-start | bytes 3145732
  44.2 6.8 %copy-start.1 = (bf16[512,1024]{1,0:T(8,128)(2,1)S(1)}, bf16[512,1024]{1,0:T(8,128)(2,1)}, u32[]{:S(2)}) copy-start(bf16[512,1024]{1,0:T(8,128)(2,1)} %near.1) | copy-start | bytes 3145732
  44.2 13.3 %collective-permute-start.4 = (bf16[256,256]{1,0:T(8,128)(2,1)S(1)}, bf16[256,256]{1,0:T(8,128)(2,1)S(1)}, u32[]{:S(2)}, u32[]{:S(2)}) collective-permute-start(bf16[256,256]{1,0:T(8,128)(2,1)S(1)} %shard_map.114.weights), channel_id=1, source_target_pairs={{511,0},{510,1},{1,2},{0,3},{2,4},{3,5},{5,6},{4,7},{7,8},{6,9},{9... | collective-permute-start | bytes 393224 | tf_op jit(solution)/shard_map/ppermute | solution.py:377
  48.5 2.5 %copy-start.4 = (bf16[256,512]{1,0:T(8,128)(2,1)S(1)}, bf16[256,512]{1,0:T(8,128)(2,1)}, u32[]{:S(2)}) copy-start(bf16[256,512]{1,0:T(8,128)(2,1)} %link.5) | copy-start | bytes 786436
